TPU v7x, 8 devices: a whole 2x2x1 slice. The times are simulated.
8 devices in a mesh: dp: 1 (over z), sp: 8 (over y, x, core).
Axes of the slice: x: 2, y: 2, z: 1, core: 2. Of those that a mesh axis runs over, the one named last changes fastest.
Arguments:
- tokens: bfloat16 [65536, 1024], P(('dp', 'sp'))
- w_q: bfloat16 [1024, 1024], replicated
- w_k: bfloat16 [1024, 1024], replicated
- w_v: bfloat16 [1024, 1024], replicated
- w_o: bfloat16 [1024, 1024], replicated
- grad_y: bfloat16 [65536, 1024], P(('dp', 'sp'))
Outputs:
- output 1: bfloat16 [65536, 1024], P(('dp', 'sp'))
- output 2: bfloat16 [65536, 1024], P(('dp', 'sp'))
- output 3: float32 [1024, 1024], P('dp')
- output 4: float32 [1024, 1024], P('dp')
- output 5: float32 [1024, 1024], P('dp')
- output 6: float32 [1024, 1024], P('dp')
All inputs are finite; a program needn't handle non-finite values.
Results may differ from a plain program's by a relative error of at most 0.00355113.
Values are sent between devices in bfloat16 or wider.
A program may use at most 1 GiB of HBM per device.

v0:
```python
import math
import jax
import jax.numpy as jnp
from jax import lax
from jax.sharding import PartitionSpec as P

HEAD_DIM = 128
BLOCK_LEN = 128


def solution(mesh):
    n_seq = mesh.shape["sp"]
    fwd_perm = [(j, j + 1) for j in range(n_seq - 1)]
    rev_perm = [(j + 1, j) for j in range(n_seq - 1)]
    row_spec = P(("dp", "sp"), None)
    grad_spec = P("dp", None)

    def local_layer(tokens, w_q, w_k, w_v, w_o, grad_y):
        n_rows, model_dim = tokens.shape
        n_heads = model_dim // HEAD_DIM
        n_blocks = n_rows // BLOCK_LEN
        att_scale = 1.0 / math.sqrt(n_rows * n_seq * HEAD_DIM)
        causal = jnp.arange(BLOCK_LEN)[:, None] >= jnp.arange(BLOCK_LEN)[None, :]

        def project(operand, weight):
            return jnp.dot(operand, weight, preferred_element_type=jnp.float32).astype(jnp.bfloat16)

        def back_proj(rows, weight):
            return jnp.einsum("ne,de->nd", rows, weight, preferred_element_type=jnp.float32)

        def weight_grad(left_rows, right_rows):
            return jnp.einsum("nd,ne->de", left_rows, right_rows, preferred_element_type=jnp.float32)

        def split_heads(tensor):
            return tensor.reshape(n_blocks, BLOCK_LEN, n_heads, HEAD_DIM)

        def to_rows(tensor):
            return (tensor * att_scale).astype(jnp.bfloat16).reshape(n_rows, model_dim)

        q_heads = split_heads(project(tokens, w_q))
        k_heads = split_heads(project(tokens, w_k))
        v_heads = split_heads(project(tokens, w_v))
        block_kv = jnp.einsum("nshd,nshe->nhde", k_heads, v_heads, preferred_element_type=jnp.float32)
        kv_total = jnp.sum(block_kv, axis=0)

        def fwd_hop(hop_index, carried):
            return lax.ppermute(carried + kv_total, "sp", perm=fwd_perm)

        kv_in = lax.fori_loop(0, n_seq - 1, fwd_hop, jnp.zeros_like(kv_total))
        fwd_state = (kv_in + jnp.cumsum(block_kv, axis=0) - block_kv).astype(jnp.bfloat16)
        scores = jnp.einsum("nthd,nshd->nhts", q_heads, k_heads, preferred_element_type=jnp.float32)
        masked_scores = jnp.where(causal, scores, 0.0).astype(jnp.bfloat16)
        out_rows = to_rows(jnp.einsum("nhts,nshe->nthe", masked_scores, v_heads, preferred_element_type=jnp.float32) + jnp.einsum("nthd,nhde->nthe", q_heads, fwd_state, preferred_element_type=jnp.float32))
        out_y = project(out_rows, w_o)

        do_heads = split_heads(back_proj(grad_y, w_o).astype(jnp.bfloat16))
        block_qdo = jnp.einsum("nthd,nthe->nhde", q_heads, do_heads, preferred_element_type=jnp.float32)
        qdo_total = jnp.sum(block_qdo, axis=0)

        def rev_hop(hop_index, carried):
            return lax.ppermute(carried + qdo_total, "sp", perm=rev_perm)

        qdo_in = lax.fori_loop(0, n_seq - 1, rev_hop, jnp.zeros_like(qdo_total))
        rev_state = (qdo_in + qdo_total - jnp.cumsum(block_qdo, axis=0)).astype(jnp.bfloat16)
        d_scores = jnp.einsum("nthe,nshe->nhts", do_heads, v_heads, preferred_element_type=jnp.float32)
        masked_grads = jnp.where(causal, d_scores, 0.0).astype(jnp.bfloat16)
        dq_rows = to_rows(jnp.einsum("nhts,nshd->nthd", masked_grads, k_heads, preferred_element_type=jnp.float32) + jnp.einsum("nthe,nhde->nthd", do_heads, fwd_state, preferred_element_type=jnp.float32))
        dk_rows = to_rows(jnp.einsum("nhts,nthd->nshd", masked_grads, q_heads, preferred_element_type=jnp.float32) + jnp.einsum("nshe,nhde->nshd", v_heads, rev_state, preferred_element_type=jnp.float32))
        dv_rows = to_rows(jnp.einsum("nhts,nthe->nshe", masked_scores, do_heads, preferred_element_type=jnp.float32) + jnp.einsum("nshd,nhde->nshe", k_heads, rev_state, preferred_element_type=jnp.float32))
        grad_x = (back_proj(dq_rows, w_q) + back_proj(dk_rows, w_k) + back_proj(dv_rows, w_v)).astype(jnp.bfloat16)
        grads = lax.psum((weight_grad(tokens, dq_rows), weight_grad(tokens, dk_rows), weight_grad(tokens, dv_rows), weight_grad(out_rows, grad_y)), "sp")
        return (out_y, grad_x) + tuple(grads)

    return jax.shard_map(local_layer, mesh=mesh, in_specs=(row_spec, P(), P(), P(), P(), row_spec), out_specs=(row_spec, row_spec, grad_spec, grad_spec, grad_spec, grad_spec), check_vma=False)
```

profile of v0, /device:TPU:0, one launch (start us, length us, event | category | flops | bytes accessed | tf_op | source)
XLA Modules:
  0.0 1176.8 jit_solution(6859299697173945606)
XLA Ops:
  7.8 21.3 %convert_bitcast_fusion.2 = bf16[1024,8,8,128]{3,1,2,0:T(8,128)(2,1)S(1)} fusion(bf16[8192,1024]{1,0:T(8,128)(2,1)} %param.10, bf16[1024,1024]{1,0:T(8,128)(2,1)} %param.11), kind=kOutput, calls=%fused_computation.30 | convolution fusion | flops 17188257792 | bytes 35651584 | tf_op jit(solution)/shard_map/dot_general | solution.py:26
  29.1 9.1 copy.61
  38.3 23.4 %copy.46 = bf16[64,128,8,128]{1,3,2,0:T(8,128)(2,1)} copy(bf16[64,128,8,128]{3,2,1,0:T(8,128)(2,1)} %bitcast.108) | data formatting | bytes 33554432 | tf_op jit(solution)/shard_map/reshape | solution.py:35
  61.7 24.0 %convert_bitcast_fusion = bf16[1024,8,8,128]{3,1,2,0:T(8,128)(2,1)} fusion(bf16[8192,1024]{1,0:T(8,128)(2,1)} %param.15, bf16[1024,1024]{1,0:T(8,128)(2,1)} %param.14), kind=kOutput, calls=%fused_computation.28 | convolution fusion | flops 17188257792 | bytes 35651584 | tf_op jit(solution)/shard_map/ne,de->nd/dot_general | solution.py:29
  85.7 15.6 %copy.64 = bf16[1024,8,8,128]{3,2,1,0:T(8,128)(2,1)} copy(bf16[1024,8,8,128]{3,1,2,0:T(8,128)(2,1)} %convert_bitcast_fusion) | data formatting | bytes 33554432
  101.4 22.7 %copy.51 = bf16[64,128,8,128]{1,3,2,0:T(8,128)(2,1)} copy(bf16[64,128,8,128]{3,2,1,0:T(8,128)(2,1)} %bitcast.109) | data formatting | bytes 33554432 | tf_op jit(solution)/shard_map/reshape | solution.py:35
  124.1 21.5 %convert_bitcast_fusion.3 = bf16[1024,8,8,128]{3,1,2,0:T(8,128)(2,1)S(1)} fusion(bf16[8192,1024]{1,0:T(8,128)(2,1)} %param.10, bf16[1024,1024]{1,0:T(8,128)(2,1)} %param.13), kind=kOutput, calls=%fused_computation.31 | convolution fusion | flops 17188257792 | bytes 35651584 | tf_op jit(solution)/shard_map/dot_general | solution.py:26
  154.7 20.6 %convert_bitcast_fusion.1 = bf16[1024,8,8,128]{3,1,2,0:T(8,128)(2,1)S(1)} fusion(bf16[8192,1024]{1,0:T(8,128)(2,1)} %param.10, bf16[1024,1024]{1,0:T(8,128)(2,1)S(1)} %copy-done), kind=kOutput, calls=%fused_computation.29 | convolution fusion | flops 17188257792 | bytes 35651584 | tf_op jit(solution)/shard_map/dot_general | solution.py:26
  175.3 9.6 copy.62
  184.9 22.7 %copy.36 = bf16[64,128,8,128]{1,3,2,0:T(8,128)(2,1)} copy(bf16[64,128,8,128]{3,2,1,0:T(8,128)(2,1)} %bitcast.105) | data formatting | bytes 33554432 | tf_op jit(solution)/shard_map/reshape | solution.py:35
  207.7 27.9 %fusion.52 = (f32[8,128,128]{2,1,0:T(8,128)S(1)}, f32[64,8,128,128]{3,2,1,0:T(8,128)}) fusion(bf16[64,128,8,128]{1,3,2,0:T(8,128)(2,1)} %copy.46, bf16[64,128,8,128]{1,3,2,0:T(8,128)(2,1)} %copy.51), kind=kOutput, calls=%fused_computation.56 | convolution fusion | flops 2155741184 | bytes 67633152 | tf_op jit(solution)/shard_map/nthd,nthe->nhde/dot_general | solution.py:57
  235.6 21.1 %select_convert_fusion.1 = bf16[64,8,128,128]{3,2,1,0:T(8,128)(2,1)} fusion(pred[128,128]{1,0:T(8,128)(4,1)S(1)} %copy-done.3, bf16[64,128,8,128]{1,3,2,0:T(8,128)(2,1)} %copy.46, bf16[64,128,8,128]{3,2,1,0:T(8,128)(2,1)} %bitcast.106), kind=kOutput, calls=%fused_computation.8 | convolution fusion | flops 2164260864 | bytes 50348032 | tf_op jit(solution)/shard_map/nthd,nshd->nhts/dot_general | solution.py:51
  256.7 21.1 %select_convert_fusion = bf16[64,8,128,128]{3,2,1,0:T(8,128)(2,1)} fusion(pred[128,128]{1,0:T(8,128)(4,1)S(1)} %copy-done.3, bf16[64,128,8,128]{1,3,2,0:T(8,128)(2,1)} %copy.51, bf16[64,128,8,128]{3,2,1,0:T(8,128)(2,1)} %bitcast.101), kind=kOutput, calls=%fused_computation.5 | convolution fusion | flops 2164260864 | bytes 50348032 | tf_op jit(solution)/shard_map/nthe,nshe->nhts/dot_general | solution.py:65
  277.8 24.4 %fusion.55 = f32[64,8,128,128]{3,2,1,0:T(8,128)} fusion(bf16[64,128,8,128]{1,3,2,0:T(8,128)(2,1)} %copy.46, bf16[64,8,128,128]{3,2,1,0:T(8,128)(2,1)} %select_convert_fusion), kind=kOutput, calls=%fused_computation.59 | convolution fusion | flops 2147483648 | bytes 67108864 | tf_op jit(solution)/shard_map/nhts,nthd->nshd/dot_general | solution.py:68
  302.2 25.6 %fusion.51 = (f32[8,128,128]{2,1,0:T(8,128)}, f32[64,8,128,128]{3,2,1,0:T(8,128)}) fusion(bf16[64,128,8,128]{1,3,2,0:T(8,128)(2,1)} %copy.36, bf16[64,128,8,128]{3,2,1,0:T(8,128)(2,1)} %bitcast.102), kind=kOutput, calls=%fused_computation.55 | convolution fusion | flops 2155741184 | bytes 67633152 | tf_op jit(solution)/shard_map/nshd,nshe->nhde/dot_general | solution.py:43
  327.8 27.8 %fusion.54 = f32[64,8,128,128]{3,2,1,0:T(8,128)} fusion(bf16[64,128,8,128]{1,3,2,0:T(8,128)(2,1)} %copy.36, bf16[64,8,128,128]{3,2,1,0:T(8,128)(2,1)} %select_convert_fusion), kind=kOutput, calls=%fused_computation.58 | convolution fusion | flops 2147483648 | bytes 67108864 | tf_op jit(solution)/shard_map/nhts,nshd->nthd/dot_general | solution.py:67
  355.7 73.9 %while.21 = (s32[]{:T(128)}, f32[8,128,128]{2,1,0:T(8,128)S(1)}, f32[8,128,128]{2,1,0:T(8,128)S(1)}, s32[]{:T(128)}) while((s32[]{:T(128)}, f32[8,128,128]{2,1,0:T(8,128)S(1)}, f32[8,128,128]{2,1,0:T(8,128)S(1)}, s32[]{:T(128)}) %tuple.42), condition=%wide.region_6.7_spmd, body=%wide.region_5.6_spmd.sunk | while | flops 131074 | bytes 3670109 | solution.py:63
  362.8 10.1 collective-permute-done.1
  375.0 9.2 collective-permute-done.1
  386.4 9.2 collective-permute-done.1
  397.7 9.2 collective-permute-done.1
  409.1 9.2 collective-permute-done.1
  420.4 9.2 collective-permute-done.1
  431.5 22.4 %fusion.53 = f32[64,8,128,128]{3,2,1,0:T(8,128)} fusion(f32[64,8,128,128]{3,2,1,0:T(8,128)} %get-tuple-element.73), kind=kOutput, calls=%fused_computation.57 | output fusion | flops 528482304 | bytes 67108864 | tf_op jit(solution)/shard_map/jit(cumsum)/reduce_window_sum | solution.py:64
  453.9 28.1 %fusion.30 = f32[64,8,128,128]{3,2,1,0:T(8,128)} fusion(bf16[64,128,8,128]{3,2,1,0:T(8,128)(2,1)} %bitcast.107, f32[64,8,128,128]{3,2,1,0:T(8,128)} %fusion.53, f32[8,128,128]{2,1,0:T(8,128)S(1)} %add.57), kind=kOutput, calls=%fused_computation.41 | convolution fusion | flops 2164260864 | bytes 84410368 | tf_op jit(solution)/shard_map/nshd,nhde->nshe/dot_general | solution.py:69
  482.0 34.0 %fusion.2 = bf16[64,128,8,128]{1,3,2,0:T(8,128)(2,1)} fusion(f32[64,8,128,128]{3,2,1,0:T(8,128)} %fusion.55, bf16[64,128,8,128]{3,2,1,0:T(8,128)(2,1)} %bitcast.103, f32[64,8,128,128]{3,2,1,0:T(8,128)} %fusion.53, f32[8,128,128]{2,1,0:T(8,128)S(1)} %add.57), kind=kOutput, calls=%fused_computation.11 | convolution fusion | flops 2189426688 | bytes 101187584 | tf_op jit(solution)/shard_map/nshe,nhde->nshd/dot_general | solution.py:68
  516.1 23.3 %copy.50 = bf16[64,128,8,128]{3,2,1,0:T(8,128)(2,1)} copy(bf16[64,128,8,128]{1,3,2,0:T(8,128)(2,1)} %fusion.2) | data formatting | bytes 33554432 | tf_op jit(solution)/shard_map/convert_element_type | solution.py:38
  539.4 24.8 %fusion.45 = f32[1024,1024]{0,1:T(8,128)} fusion(bf16[8192,1024]{1,0:T(8,128)(2,1)} %param.10, bf16[1024,8,8,128]{3,2,1,0:T(8,128)(2,1)} %bitcast.110), kind=kOutput, calls=%fused_computation.52 | convolution fusion | flops 17179869184 | bytes 37748736 | tf_op jit(solution)/shard_map/nd,ne->de/dot_general | solution.py:32
  564.2 25.2 %fusion.34 = f32[64,8,128,128]{3,2,1,0:T(8,128)} fusion(bf16[64,8,128,128]{3,2,1,0:T(8,128)(2,1)} %select_convert_fusion.1, bf16[64,128,8,128]{3,2,1,0:T(8,128)(2,1)} %bitcast.104), kind=kOutput, calls=%fused_computation.45 | convolution fusion | flops 2147483648 | bytes 67108864 | tf_op jit(solution)/shard_map/nhts,nshe->nthe/dot_general | solution.py:53
  589.4 27.7 %fusion.3 = bf16[64,128,8,128]{1,3,2,0:T(8,128)(2,1)} fusion(f32[64,8,128,128]{3,2,1,0:T(8,128)} %fusion.30, bf16[64,128,8,128]{1,3,2,0:T(8,128)(2,1)} %copy.51, bf16[64,8,128,128]{3,2,1,0:T(8,128)(2,1)} %select_convert_fusion.1), kind=kOutput, calls=%fused_computation.12 | convolution fusion | flops 2172649472 | bytes 83886080 | tf_op jit(solution)/shard_map/nhts,nthe->nshe/dot_general | solution.py:69
  617.1 23.3 %copy.54 = bf16[64,128,8,128]{3,2,1,0:T(8,128)(2,1)} copy(bf16[64,128,8,128]{1,3,2,0:T(8,128)(2,1)} %fusion.3) | data formatting | bytes 33554432 | tf_op jit(solution)/shard_map/convert_element_type | solution.py:38
  640.4 24.9 %fusion.48 = f32[1024,1024]{0,1:T(8,128)} fusion(bf16[8192,1024]{1,0:T(8,128)(2,1)} %param.10, bf16[1024,8,8,128]{3,2,1,0:T(8,128)(2,1)} %bitcast.112), kind=kOutput, calls=%fused_computation.53 | convolution fusion | flops 17179869184 | bytes 37748736 | tf_op jit(solution)/shard_map/nd,ne->de/dot_general | solution.py:32
  665.4 78.0 %while.20 = (s32[]{:T(128)}, f32[8,128,128]{2,1,0:T(8,128)S(1)}, f32[8,128,128]{2,1,0:T(8,128)S(1)}, s32[]{:T(128)}) while((s32[]{:T(128)}, f32[8,128,128]{2,1,0:T(8,128)S(1)}, f32[8,128,128]{2,1,0:T(8,128)S(1)}, s32[]{:T(128)}) %tuple.49), condition=%wide.region_2.0_spmd, body=%wide.region_1.0_spmd.sunk | while | flops 131074 | bytes 3670109 | solution.py:49
  666.3 9.1 collective-permute-start
  686.6 9.8 collective-permute-start
  732.7 9.2 collective-permute-start
  743.4 27.6 %subtract_convert_fusion.1 = bf16[64,8,128,128]{3,2,1,0:T(8,128)(2,1)} fusion(f32[64,8,128,128]{3,2,1,0:T(8,128)} %get-tuple-element.71, f32[8,128,128]{2,1,0:T(8,128)S(1)} %get-tuple-element.40), kind=kOutput, calls=%fused_computation.7 | output fusion | flops 553648128 | bytes 50855936 | tf_op jit(solution)/shard_map/jit(cumsum)/reduce_window_sum | solution.py:50
  771.0 27.7 %fusion.1 = bf16[64,128,8,128]{1,3,2,0:T(8,128)(2,1)} fusion(f32[64,8,128,128]{3,2,1,0:T(8,128)} %fusion.54, bf16[64,8,128,128]{3,2,1,0:T(8,128)(2,1)} %subtract_convert_fusion.1, bf16[64,128,8,128]{1,3,2,0:T(8,128)(2,1)} %copy.51), kind=kOutput, calls=%fused_computation.10 | convolution fusion | flops 2172649472 | bytes 83886080 | tf_op jit(solution)/shard_map/nthe,nhde->nthd/dot_general | solution.py:67
  798.7 22.7 %copy.45 = bf16[64,128,8,128]{3,2,1,0:T(8,128)(2,1)} copy(bf16[64,128,8,128]{1,3,2,0:T(8,128)(2,1)} %fusion.1) | data formatting | bytes 33554432 | tf_op jit(solution)/shard_map/convert_element_type | solution.py:38
  821.5 24.7 %fusion.42 = f32[1024,1024]{0,1:T(8,128)} fusion(bf16[8192,1024]{1,0:T(8,128)(2,1)} %param.10, bf16[1024,8,8,128]{3,2,1,0:T(8,128)(2,1)} %bitcast.114), kind=kOutput, calls=%fused_computation.51 | convolution fusion | flops 17179869184 | bytes 37748736 | tf_op jit(solution)/shard_map/nd,ne->de/dot_general | solution.py:32
  846.2 28.6 %fusion = bf16[64,128,8,128]{1,3,2,0:T(8,128)(2,1)} fusion(f32[64,8,128,128]{3,2,1,0:T(8,128)} %fusion.34, bf16[64,8,128,128]{3,2,1,0:T(8,128)(2,1)} %subtract_convert_fusion.1, bf16[64,128,8,128]{1,3,2,0:T(8,128)(2,1)} %copy.46), kind=kOutput, calls=%fused_computation.9 | convolution fusion | flops 2172649472 | bytes 83886080 | tf_op jit(solution)/shard_map/nthd,nhde->nthe/dot_general | solution.py:53
  874.8 23.3 %copy.40 = bf16[64,128,8,128]{3,2,1,0:T(8,128)(2,1)} copy(bf16[64,128,8,128]{1,3,2,0:T(8,128)(2,1)} %fusion) | data formatting | bytes 33554432 | tf_op jit(solution)/shard_map/convert_element_type | solution.py:38
  898.1 24.6 %fusion.15 = f32[1024,1024]{1,0:T(8,128)} fusion(bf16[8192,1024]{1,0:T(8,128)(2,1)} %param.15, bf16[1024,8,8,128]{3,2,1,0:T(8,128)(2,1)} %bitcast.116), kind=kOutput, calls=%fused_computation.24 | convolution fusion | flops 17179869184 | bytes 37748736 | tf_op jit(solution)/shard_map/nd,ne->de/dot_general | solution.py:32
  922.7 25.7 %fusion.9 = f32[8192,1024]{1,0:T(8,128)} fusion(bf16[1024,1024]{1,0:T(8,128)(2,1)S(1)} %copy-done, bf16[1024,8,8,128]{3,2,1,0:T(8,128)(2,1)} %bitcast.111), kind=kOutput, calls=%fused_computation.18 | convolution fusion | flops 17179869184 | bytes 52428800 | tf_op jit(solution)/shard_map/ne,de->nd/dot_general | solution.py:29
  948.4 25.5 %fusion.13 = f32[8192,1024]{1,0:T(8,128)} fusion(bf16[1024,1024]{1,0:T(8,128)(2,1)S(1)} %copy-done.4, bf16[1024,8,8,128]{3,2,1,0:T(8,128)(2,1)} %bitcast.115), kind=kOutput, calls=%fused_computation.22 | convolution fusion | flops 17179869184 | bytes 52428800 | tf_op jit(solution)/shard_map/ne,de->nd/dot_general | solution.py:29
  973.9 26.2 %fusion.19 = bf16[8192,1024]{1,0:T(8,128)(2,1)} fusion(bf16[1024,1024]{1,0:T(8,128)(2,1)S(1)} %copy-done.5, bf16[1024,8,8,128]{3,2,1,0:T(8,128)(2,1)} %bitcast.117), kind=kOutput, calls=%fused_computation.32 | convolution fusion | flops 17188257792 | bytes 35651584 | tf_op jit(solution)/shard_map/dot_general | solution.py:26
  1000.1 36.8 %add_convert_fusion = bf16[8192,1024]{1,0:T(8,128)(2,1)} fusion(f32[8192,1024]{1,0:T(8,128)} %fusion.13, f32[8192,1024]{1,0:T(8,128)} %fusion.9, bf16[1024,1024]{1,0:T(8,128)(2,1)} %param.13, bf16[1024,8,8,128]{3,2,1,0:T(8,128)(2,1)} %bitcast.113), kind=kOutput, calls=%fused_computation | convolution fusion | flops 17205035008 | bytes 102760448 | tf_op jit(solution)/shard_map/ne,de->nd/dot_general | solution.py:29
  1036.9 111.8 %all-reduce.3.cloned.1.call-done = (f32[1024,1024]{0,1:T(8,128)}, f32[1024,1024]{0,1:T(8,128)}, f32[1024,1024]{0,1:T(8,128)}, f32[1024,1024]{1,0:T(8,128)}) async-done(((f32[1024,1024]{0,1:T(8,128)}, f32[1024,1024]{0,1:T(8,128)}, f32[1024,1024]{0,1:T(8,128)}, f32[1024,1024]{1,0:T(8,128)}), (f32[1024,1024]{0,1:T(8,128)}, f32[1024,1024]{0,1:T(8,128)}, f32[1024,1024]{0,1:T(8,128)}, ...) | async-done | bytes 16777232 | tf_op jit(solution)/shard_map/psum | solution.py:71
  (56 shorter events, 100.1 us)
Async XLA Ops:
  7.2 147.5 %copy-start = (bf16[1024,1024]{1,0:T(8,128)(2,1)S(1)}, bf16[1024,1024]{1,0:T(8,128)(2,1)}, u32[]{:S(2)}) copy-start(bf16[1024,1024]{1,0:T(8,128)(2,1)} %param.12) | copy-start | bytes 6291460
  7.2 1141.6 %all-reduce.3.cloned.1.call-start = ((), (), s32[]{:S(2)}) async-start(), calls=%async_computation | async-start | bytes 33554432 | tf_op jit(solution)/shard_map/psum | solution.py:71
  207.7 27.9 %copy-start.3 = (pred[128,128]{1,0:T(8,128)(4,1)S(1)}, pred[128,128]{1,0:T(8,128)(4,1)}, u32[]{:S(2)}) copy-start(pred[128,128]{1,0:T(8,128)(4,1)} %iota_compare_fusion) | copy-start | bytes 49156
  356.5 4.1 collective-permute-start.1
  361.5 11.4 collective-permute-start.1
  373.7 10.5 collective-permute-start.1
  385.1 10.5 collective-permute-start.1
  396.4 10.5 collective-permute-start.1
  407.8 10.5 collective-permute-start.1
  419.1 10.5 collective-permute-start.1
  429.6 0.8 copy-start.1
  640.4 25.0 %copy-start.2 = (f32[8,128,128]{2,1,0:T(8,128)S(1)}, f32[8,128,128]{2,1,0:T(8,128)}, u32[]{:S(2)}) copy-start(f32[8,128,128]{2,1,0:T(8,128)} %get-tuple-element.114) | copy-start | bytes 1572868
  666.3 10.6 collective-permute-start
  677.7 8.0 collective-permute-start
  686.6 11.3 collective-permute-start
  698.7 10.5 collective-permute-start
  710.1 10.5 collective-permute-start
  721.4 10.5 collective-permute-start
  732.7 10.7 collective-permute-start
  922.7 25.7 %copy-start.4 = (bf16[1024,1024]{1,0:T(8,128)(2,1)S(1)}, bf16[1024,1024]{1,0:T(8,128)(2,1)}, u32[]{:S(2)}) copy-start(bf16[1024,1024]{1,0:T(8,128)(2,1)} %param.11) | copy-start | bytes 6291460
  948.4 25.5 %copy-start.5 = (bf16[1024,1024]{1,0:T(8,128)(2,1)S(1)}, bf16[1024,1024]{1,0:T(8,128)(2,1)}, u32[]{:S(2)}) copy-start(bf16[1024,1024]{1,0:T(8,128)(2,1)} %param.14) | copy-start | bytes 6291460
Sparse Core Ops, SparseCore 0:
  922.8 225.8 all-reduce.2
where the time goes:
time: 1190 us; the launch traced here: 1180 us
  matrix products  620 us (52%)
  local copies, waits for them, and re-layouts  227 us (19%)
  waiting for transfers between devices  181 us (15%)
  starting transfers between devices  70.6 us (6%)
  other arithmetic  63.6 us (5%)
  between operations  14.5 us (1%)
    dot_general x4, matrix products, back_proj(): jnp.einsum('ne,de->nd', rows, weight, preferred_element_type=jnp.float32)  112 us
    psum x1, waiting for transfers between devices, local_layer(): lax.psum((weight_grad(tokens, dq_rows), weight_grad(tokens, dk_rows), wei...  112 us
    dot_general x4, matrix products, weight_grad(): jnp.einsum('nd,ne->de', left_rows, right_rows, preferred_element_type=jnp...  99 us
    convert_element_type x4, local copies, waits for them, and re-layouts, to_rows(): return (tensor * att_scale).astype(jnp.bfloat16).reshape(n_rows, model_dim)  92.7 us
    dot_general x4, matrix products, project(): jnp.dot(operand, weight, preferred_element_type=jnp.float32)  89.6 us
    reshape x3, local copies, waits for them, and re-layouts, split_heads(): return tensor.reshape(n_blocks, BLOCK_LEN, n_heads, HEAD_DIM)  68.8 us
    unnamed x20, local copies, waits for them, and re-layouts  65.1 us
    ppermute x7, starting transfers between devices, fwd_hop(): return lax.ppermute(carried + kv_total, 'sp', perm=fwd_perm)  61.6 us
  transfers between devices with their start and end apart: 15, of which 15 were waited for; matrix products, arithmetic and copies ran while one was open for 10% of the time, Pallas kernels for 0%

commit v1 on v0

v1 whole, which is shorter than its diff:
```python
import functools
import math
import jax
import jax.numpy as jnp
from jax import lax
from jax.experimental import pallas as pl
from jax.experimental.pallas import tpu as pltpu
from jax.sharding import PartitionSpec as P

HEAD_DIM = 128
BLOCK_LEN = 128
GROUPS = 2

F32 = jnp.float32
BF16 = jnp.bfloat16


def dot_nn(a, b):
    return jnp.dot(a, b, preferred_element_type=F32)


def dot_nt(a, b):
    return lax.dot_general(a, b, (((1,), (1,)), ((), ())), preferred_element_type=F32)


def dot_tn(a, b):
    return lax.dot_general(a, b, (((0,), (0,)), ((), ())), preferred_element_type=F32)


def proj_kernel(x_ref, dy_ref, wq_ref, wk_ref, wv_ref, wo_ref, q_ref, k_ref, v_ref, g_ref, tot_ref):
    @pl.when(pl.program_id(0) == 0)
    def _():
        tot_ref[...] = jnp.zeros_like(tot_ref)

    q_ref[...] = dot_nn(x_ref[...], wq_ref[...]).astype(BF16)
    k_ref[...] = dot_nn(x_ref[...], wk_ref[...]).astype(BF16)
    v_ref[...] = dot_nn(x_ref[...], wv_ref[...]).astype(BF16)
    g_ref[...] = dot_nt(dy_ref[...], wo_ref[...]).astype(BF16)
    for h in range(tot_ref.shape[1]):
        cols = slice(h * HEAD_DIM, (h + 1) * HEAD_DIM)
        tot_ref[0, h] += dot_tn(k_ref[:, cols], v_ref[:, cols])
        tot_ref[1, h] += dot_tn(q_ref[:, cols], g_ref[:, cols])


def project(tokens, grad_y, w_q, w_k, w_v, w_o, group, tile):
    n_rows, dim = tokens.shape
    cols = dim // GROUPS
    heads = cols // HEAD_DIM
    row_in = pl.BlockSpec((tile, dim), lambda i: (i, 0))
    w_in = pl.BlockSpec((dim, cols), lambda i: (0, group))
    row_out = pl.BlockSpec((tile, cols), lambda i: (i, 0))
    rows = jax.ShapeDtypeStruct((n_rows, cols), BF16)
    return pl.pallas_call(
        proj_kernel,
        grid=(n_rows // tile,),
        in_specs=[row_in, row_in, w_in, w_in, w_in, pl.BlockSpec((cols, dim), lambda i: (group, 0))],
        out_specs=[row_out] * 4 + [pl.BlockSpec((2, heads, HEAD_DIM, HEAD_DIM), lambda i: (0, 0, 0, 0))],
        out_shape=[rows] * 4 + [jax.ShapeDtypeStruct((2, heads, HEAD_DIM, HEAD_DIM), F32)],
        cost_estimate=pl.CostEstimate(flops=8 * n_rows * dim * cols, bytes_accessed=2 * n_rows * (2 * dim + 4 * cols), transcendentals=0),
        name=f"project{group}",
    )(tokens, grad_y, w_q, w_k, w_v, w_o)


def attn_kernel(scale, q_ref, k_ref, v_ref, g_ref, tot_ref, o_ref, dq_ref, dk_ref, dv_ref, s_ref, r_ref, a_ref, at_ref, c_ref, ct_ref, sb_ref, st_ref, rb_ref, rt_ref):
    n_heads = s_ref.shape[0]

    @pl.when(pl.program_id(0) == 0)
    def _():
        me = lax.axis_index("sp")
        for h in range(n_heads):
            s_ref[h] = jnp.zeros_like(s_ref[h])
            r_ref[h] = jnp.zeros_like(r_ref[h])
            for d in range(tot_ref.shape[0]):
                s_ref[h] += jnp.where(d < me, tot_ref[d, 0, h], 0.0)
                r_ref[h] += jnp.where(d >= me, tot_ref[d, 1, h], 0.0)

    causal = lax.broadcasted_iota(jnp.int32, (BLOCK_LEN, BLOCK_LEN), 0) >= lax.broadcasted_iota(jnp.int32, (BLOCK_LEN, BLOCK_LEN), 1)
    units = [(b, h) for b in range(q_ref.shape[0] // BLOCK_LEN) for h in range(n_heads)]

    def load(b, h):
        rows = slice(b * BLOCK_LEN, (b + 1) * BLOCK_LEN)
        cols = slice(h * HEAD_DIM, (h + 1) * HEAD_DIM)
        return rows, cols, q_ref[rows, cols], k_ref[rows, cols], v_ref[rows, cols], g_ref[rows, cols]

    for i, (b, h) in enumerate(units):
        _, _, q, k, v, g = load(b, h)
        kt = k.T
        a = jnp.where(causal, dot_nn(q, kt), 0.0).astype(BF16)
        c = jnp.where(causal, dot_nn(g, v.T), 0.0).astype(BF16)
        a_ref[i] = a
        c_ref[i] = c
        at_ref[i] = a.T
        ct_ref[i] = c.T
        s = s_ref[h]
        r = r_ref[h] - dot_nn(q.T, g)
        s_ref[h] = s + dot_nn(kt, v)
        r_ref[h] = r
        s = s.astype(BF16)
        r = r.astype(BF16)
        sb_ref[i] = s
        st_ref[i] = s.T
        rb_ref[i] = r
        rt_ref[i] = r.T

    def pair(left, left_state, right, right_state):
        return dot_nn(jnp.concatenate([left, left_state], axis=1), jnp.concatenate([right, right_state], axis=0)) * scale

    for i, (b, h) in enumerate(units):
        rows, cols, q, k, v, g = load(b, h)
        o_ref[rows, cols] = pair(a_ref[i], q, v, sb_ref[i]).astype(BF16)
        dq_ref[rows, cols] = pair(c_ref[i], g, k, st_ref[i]).astype(BF16)
        dk_ref[rows, cols] = pair(ct_ref[i], v, q, rt_ref[i]).astype(BF16)
        dv_ref[rows, cols] = pair(at_ref[i], k, g, rb_ref[i]).astype(BF16)


def attend(q, k, v, g, totals, scale, group, tile):
    n_rows, cols = q.shape
    heads = cols // HEAD_DIM
    row_spec = pl.BlockSpec((tile, cols), lambda i: (i, 0))
    state = (heads, HEAD_DIM, HEAD_DIM)
    units = (tile // BLOCK_LEN * heads, BLOCK_LEN, BLOCK_LEN)
    return pl.pallas_call(
        functools.partial(attn_kernel, scale),
        grid=(n_rows // tile,),
        in_specs=[row_spec] * 4 + [pl.BlockSpec(totals.shape, lambda i: (0, 0, 0, 0, 0))],
        out_specs=[row_spec] * 4,
        out_shape=[jax.ShapeDtypeStruct((n_rows, cols), BF16)] * 4,
        scratch_shapes=[pltpu.VMEM(state, F32)] * 2 + [pltpu.VMEM(units, BF16)] * 8,
        cost_estimate=pl.CostEstimate(flops=64 * n_rows * cols * HEAD_DIM, bytes_accessed=16 * n_rows * cols, transcendentals=0),
        name=f"attend{group}",
    )(q, k, v, g, totals)


def wgrad_kernel(x_ref, dy_ref, o_ref, dq_ref, dk_ref, dv_ref, grad_ref):
    @pl.when(pl.program_id(0) == 0)
    def _():
        grad_ref[...] = jnp.zeros_like(grad_ref)

    xt = x_ref[...].T
    grad_ref[0] += dot_nn(xt, dq_ref[...])
    grad_ref[1] += dot_nn(xt, dk_ref[...])
    grad_ref[2] += dot_nn(xt, dv_ref[...])
    cols = o_ref.shape[1]
    grad_o = dot_tn(o_ref[...], dy_ref[...])
    for part in range(GROUPS):
        grad_ref[3, part * cols:(part + 1) * cols] += grad_o[:, part * cols:(part + 1) * cols]


def weight_grads(tokens, grad_y, o, dq, dk, dv, group, tile):
    n_rows, dim = tokens.shape
    cols = o.shape[1]
    wide = pl.BlockSpec((tile, dim), lambda i: (i, 0))
    half = pl.BlockSpec((tile, cols), lambda i: (i, 0))
    return pl.pallas_call(
        wgrad_kernel,
        grid=(n_rows // tile,),
        in_specs=[wide, wide] + [half] * 4,
        out_specs=pl.BlockSpec((4, dim, cols), lambda i: (0, 0, 0)),
        out_shape=jax.ShapeDtypeStruct((4, dim, cols), F32),
        cost_estimate=pl.CostEstimate(flops=8 * n_rows * dim * cols, bytes_accessed=2 * n_rows * (2 * dim + 4 * cols), transcendentals=0),
        name=f"wgrad{group}",
    )(tokens, grad_y, o, dq, dk, dv)


def add_rows(dst, start, src):
    step = 64

    def body(i, carry):
        there = pl.ds(pl.multiple_of(start + i * step, step), step)
        dst[there, :] += src[pl.ds(pl.multiple_of(i * step, step), step), :]
        return carry

    lax.fori_loop(0, src.shape[0] // step, body, 0)


def reduce_kernel(marks, dq0_ref, dq1_ref, dk0_ref, dk1_ref, wq_ref, wk_ref, grad_ref, part_ref, shard_ref, own, got, got_x, got_y, end_x, end_y, send_sem, recv_sem, local_sem):
    step = pl.program_id(0)
    me = lax.axis_index("sp")
    core, x, y = me % 2, (me // 2) % 2, (me // 4) % 2
    peer_core, peer_x, peer_y = me + 1 - 2 * core, me + 2 - 4 * x, me + 4 - 8 * y
    half = own.shape[0]
    quarter, eighth, last = half // 2, half // 4, half // 8

    def rows(ref, start, size):
        return ref.at[pl.ds(pl.multiple_of(start, last), size), :]

    def remote(i, src, dst, peer):
        return pltpu.make_async_remote_copy(src_ref=src, dst_ref=dst, send_sem=send_sem.at[i], recv_sem=recv_sem.at[i], device_id={"sp": peer}, device_id_type=pl.DeviceIdType.MESH)

    keep_x, keep_y = x * eighth, quarter + y * eighth
    swap = remote(0, rows(grad_ref, (1 - core) * half, half), got, peer_core)
    local = pltpu.make_async_copy(rows(grad_ref, core * half, half), own, local_sem)
    first_x = remote(1, rows(own, (1 - x) * eighth, eighth), got_x, peer_x)
    first_y = remote(2, rows(own, quarter + (1 - y) * eighth, eighth), got_y, peer_y)
    second_x = remote(3, rows(own, keep_x + (1 - y) * last, last), end_x, peer_y)
    second_y = remote(4, rows(own, keep_y + (1 - x) * last, last), end_y, peer_x)

    @pl.when(step == 0)
    def _():
        barrier = pltpu.get_barrier_semaphore()
        for peer in (peer_core, peer_x, peer_y):
            pl.semaphore_signal(barrier, inc=1, device_id={"sp": peer}, device_id_type=pl.DeviceIdType.MESH)
        pl.semaphore_wait(barrier, 3)
        swap.start()
        local.start()

    @pl.when(step == marks[0])
    def _():
        local.wait()
        swap.wait()
        add_rows(own, 0, got)

    @pl.when(step == marks[1])
    def _():
        first_x.wait()
        first_y.wait()
        add_rows(own, keep_x, got_x)
        add_rows(own, keep_y, got_y)

    dq = jnp.concatenate([dq0_ref[...], dq1_ref[...]], axis=1)
    dk = jnp.concatenate([dk0_ref[...], dk1_ref[...]], axis=1)
    part_ref[...] = dot_nt(dq, wq_ref[...]) + dot_nt(dk, wk_ref[...])

    @pl.when(step == marks[0])
    def _():
        first_x.start()
        first_y.start()

    @pl.when(step == marks[1])
    def _():
        second_x.start()
        second_y.start()

    @pl.when(step == pl.num_programs(0) - 1)
    def _():
        second_x.wait()
        second_y.wait()
        shard_ref[0] = own[pl.ds(pl.multiple_of(keep_x + y * last, last), last), :] + end_x[...]
        shard_ref[1] = own[pl.ds(pl.multiple_of(keep_y + x * last, last), last), :] + end_y[...]


def reduce_beside(parts, w_q, w_k, grads, tile, marks):
    n_rows, cols = parts[0].shape
    dim = w_q.shape[0]
    total = grads.shape[0] * grads.shape[1]
    half = pl.BlockSpec((tile, cols), lambda i: (i, 0))
    weight = pl.BlockSpec((dim, dim), lambda i: (0, 0))
    shard = (2, total // 16, cols)
    sizes = [total // 2, total // 2, total // 8, total // 8, total // 16, total // 16]
    return pl.pallas_call(
        functools.partial(reduce_kernel, marks),
        grid=(n_rows // tile,),
        in_specs=[half] * 4 + [weight] * 2 + [pl.BlockSpec(memory_space=pl.ANY)],
        out_specs=[pl.BlockSpec((tile, dim), lambda i: (i, 0)), pl.BlockSpec(shard, lambda i: (0, 0, 0))],
        out_shape=[jax.ShapeDtypeStruct((n_rows, dim), F32), jax.ShapeDtypeStruct(shard, F32)],
        scratch_shapes=[pltpu.VMEM((size, cols), F32) for size in sizes] + [pltpu.SemaphoreType.DMA((5,))] * 2 + [pltpu.SemaphoreType.DMA],
        compiler_params=pltpu.CompilerParams(collective_id=0, has_side_effects=True),
        cost_estimate=pl.CostEstimate(flops=4 * n_rows * dim * dim, bytes_accessed=8 * n_rows * dim, transcendentals=0),
        name="reduce_beside",
    )(*parts, w_q, w_k, grads.reshape(total, cols))


def out_kernel(o0_ref, o1_ref, dv0_ref, dv1_ref, part_ref, wo_ref, wv_ref, grad_ref, y_ref, dx_ref, gq_ref, gk_ref, gv_ref, go_ref):
    y_ref[...] = dot_nn(jnp.concatenate([o0_ref[...], o1_ref[...]], axis=1), wo_ref[...]).astype(BF16)
    dv = jnp.concatenate([dv0_ref[...], dv1_ref[...]], axis=1)
    dx_ref[...] = (part_ref[...] + dot_nt(dv, wv_ref[...])).astype(BF16)
    for i, ref in enumerate((gq_ref, gk_ref, gv_ref, go_ref)):
        ref[...] = grad_ref[i]


def back_project(parts, partial, w_o, w_v, grads, tile):
    n_rows, cols = parts[0].shape
    dim = w_o.shape[1]
    steps = n_rows // tile
    piece = dim // steps
    down = cols // piece
    half = pl.BlockSpec((tile, cols), lambda i: (i, 0))
    weight = pl.BlockSpec((dim, dim), lambda i: (0, 0))
    row_out = pl.BlockSpec((tile, dim), lambda i: (i, 0))
    left = pl.BlockSpec((piece, cols), lambda i: (i, 0))
    return pl.pallas_call(
        out_kernel,
        grid=(steps,),
        in_specs=[half] * 4 + [row_out] + [weight] * 2 + [pl.BlockSpec((4, piece, cols), lambda i: (0, i, 0))],
        out_specs=[row_out] * 2 + [left] * 3 + [pl.BlockSpec((piece, cols), lambda i: (i % down, i // down))],
        out_shape=[jax.ShapeDtypeStruct((n_rows, dim), BF16)] * 2 + [jax.ShapeDtypeStruct((dim, dim), F32)] * 4,
        cost_estimate=pl.CostEstimate(flops=4 * n_rows * dim * dim, bytes_accessed=12 * n_rows * dim, transcendentals=0),
        name="back_project",
    )(*parts, partial, w_o, w_v, grads)


def place_kernel(s0_ref, s1_ref, s2_ref, s3_ref, a0_ref, a1_ref, a2_ref, a3_ref, gq_ref, gk_ref, gv_ref, go_ref):
    for src, dst in ((s0_ref, gq_ref), (s1_ref, gk_ref), (s2_ref, gv_ref), (s3_ref, go_ref)):
        dst[...] = src[0, 0]


def place(gathered, grads):
    piece, cols = gathered.shape[2:]
    down = cols // piece

    def source(slot):
        if slot % 2:
            return lambda i: (i * 2 + slot // 2, 1, 0, 0)
        return lambda i: (((i % 2) * 2 + i // 2) * 2 + slot // 2, 0, 0, 0)

    right = pl.BlockSpec((piece, cols), lambda i: (i, 1))
    return pl.pallas_call(
        place_kernel,
        grid=(4,),
        in_specs=[pl.BlockSpec((1, 1, piece, cols), source(slot)) for slot in range(4)] + [pl.BlockSpec(memory_space=pl.ANY)] * 4,
        out_specs=[right] * 3 + [pl.BlockSpec((piece, cols), lambda i: (down + i % down, i // down))],
        out_shape=[jax.ShapeDtypeStruct(g.shape, g.dtype) for g in grads],
        input_output_aliases={4 + i: i for i in range(4)},
        cost_estimate=pl.CostEstimate(flops=0, bytes_accessed=8 * gathered.size, transcendentals=0),
        name="place",
    )(*[gathered] * 4, *grads)


def solution(mesh):
    n_seq = mesh.shape["sp"]
    row_spec = P(("dp", "sp"), None)
    grad_spec = P("dp", None)

    def local_layer(tokens, w_q, w_k, w_v, w_o, grad_y):
        scale = 1.0 / math.sqrt(tokens.shape[0] * n_seq * HEAD_DIM)
        projected = [project(tokens, grad_y, w_q, w_k, w_v, w_o, g, 1024) for g in range(GROUPS)]
        gathered = [lax.all_gather(p[4], "sp") for p in projected]
        parts = [None] * GROUPS
        parts[0] = attend(*projected[0][:4], gathered[0], scale, 0, 512)
        first = lax.psum(weight_grads(tokens, grad_y, *parts[0], 0, 1024), "sp")
        parts[1] = attend(*projected[1][:4], gathered[1], scale, 1, 512)
        second = weight_grads(tokens, grad_y, *parts[1], 1, 1024)
        o, dq, dk, dv = zip(*parts)
        partial, shard = reduce_beside(dq + dk, w_q, w_k, second, 512, (3, 13))
        shards = lax.all_gather(shard, "sp")
        out_y, grad_x, *grads = back_project(o + dv, partial, w_o, w_v, first, 512)
        return (out_y, grad_x) + tuple(place(shards, grads))

    return jax.shard_map(local_layer, mesh=mesh, in_specs=(row_spec, P(), P(), P(), P(), row_spec), out_specs=(row_spec, row_spec, grad_spec, grad_spec, grad_spec, grad_spec), check_vma=False)
```

time: 1190 us -> 404 us (0.34); the launches traced: 1180 us -> 403 us
  matrix products: 620 us -> 0 us
  Pallas kernels: 0 us -> 388 us
  local copies, waits for them, and re-layouts: 227 us -> 0 us
  waiting for transfers between devices: 181 us -> 0.15 us
  starting transfers between devices: 70.6 us -> 0.56 us
  other arithmetic: 63.6 us -> 0 us
    dot_general x24 -> x0, matrix products: 620 us -> none  [the longest x4 112 us: back_proj(): jnp.einsum('ne,de->nd', rows, weight, preferred_element_type=jnp.float32)]
    pallas_call x0 -> x9, Pallas kernels: none -> 388 us  [the longest x2 92 us: project(): pl.pallas_call(proj_kernel, grid=(n_rows // tile,), in_specs=[row_in, row...]
    psum x1, waiting for transfers between devices: 112 us -> 0.02 us  [local_layer(): first = lax.psum(weight_grads(tokens, grad_y, *parts[0], 0, 1024), 'sp')]
    convert_element_type x4 -> x0, local copies, waits for them, and re-layouts: 92.7 us -> none  [to_rows(): return (tensor * att_scale).astype(jnp.bfloat16).reshape(n_rows, model_dim)]
    ppermute x14 -> x0, starting transfers between devices: 70.5 us -> none  [the longest x7 61.6 us: fwd_hop(): return lax.ppermute(carried + kv_total, 'sp', perm=fwd_perm)]
    ppermute x14 -> x0, waiting for transfers between devices: 69.3 us -> none  [the longest x7 58.9 us: rev_hop(): return lax.ppermute(carried + qdo_total, 'sp', perm=rev_perm)]
    reshape x3 -> x0, local copies, waits for them, and re-layouts: 68.8 us -> none  [split_heads(): return tensor.reshape(n_blocks, BLOCK_LEN, n_heads, HEAD_DIM)]
    unnamed x20 -> x0, local copies, waits for them, and re-layouts: 65.1 us -> none
  transfers between devices with their start and end apart: 15 -> 4, of which waited for: 15 -> 0; matrix products, arithmetic and copies ran while one was open for 10% -> 0% of each run, Pallas kernels for 0% -> 83%
where the time goes in v1:
time: 404 us; the launch traced here: 403 us
  Pallas kernels  388 us (96%)
  between operations  13.8 us (3%)
    pallas_call x2, Pallas kernels, project(): pl.pallas_call(proj_kernel, grid=(n_rows // tile,), in_specs=[row_in, row...  92 us
    pallas_call x2, Pallas kernels, weight_grads(): pl.pallas_call(wgrad_kernel, grid=(n_rows // tile,), in_specs=[wide, wide...  87.5 us
    pallas_call x2, Pallas kernels, attend(): pl.pallas_call(functools.partial(attn_kernel, scale), grid=(n_rows // til...  78.4 us
    pallas_call x1, Pallas kernels, reduce_beside(): pl.pallas_call(functools.partial(reduce_kernel, marks), grid=(n_rows // t...  74.5 us
    pallas_call x1, Pallas kernels, back_project(): pl.pallas_call(out_kernel, grid=(steps,), in_specs=[half] * 4 + [row_out]...  48.8 us
  transfers between devices with their start and end apart: 4, of which 0 were waited for; matrix products, arithmetic and copies ran while one was open for 0% of the time, Pallas kernels for 83%

profile of v1, /device:TPU:0, one launch (start us, length us, event | category | flops | bytes accessed | tf_op | source)
XLA Modules:
  0.0 402.8 jit_solution(8071880238227235744)
XLA Ops:
  7.2 0.0 all-gather.7.cloned.1.call-start
  7.2 46.0 %project0.1 = (bf16[8192,512]{1,0:T(8,128)(2,1)}, bf16[8192,512]{1,0:T(8,128)(2,1)}, bf16[8192,512]{1,0:T(8,128)(2,1)}, bf16[8192,512]{1,0:T(8,128)(2,1)}, f32[2,4,128,128]{3,2,1,0:T(8,128)}) custom-call(bf16[8192,1024]{1,0:T(8,128)(2,1)} %x_ref.7, bf16[8192,1024]{1,0:T(8,128)(2,1)} %dy_ref.7, bf16[1024,1024]{1,0:T(8,128)(2,1)} %wq_ref.5, ...), custom_call_target="tpu_custom_call" | custom-call | flops 34359738368 | bytes 67108864 | tf_op jit(solution)/shard_map/project0/pallas_call | solution.py:53
  53.2 0.0 all-gather.7.cloned.1.call-update
  53.2 0.0 all-gather.9.cloned.1.call-start
  53.3 46.0 %project1.1 = (bf16[8192,512]{1,0:T(8,128)(2,1)}, bf16[8192,512]{1,0:T(8,128)(2,1)}, bf16[8192,512]{1,0:T(8,128)(2,1)}, bf16[8192,512]{1,0:T(8,128)(2,1)}, f32[2,4,128,128]{3,2,1,0:T(8,128)}) custom-call(bf16[8192,1024]{1,0:T(8,128)(2,1)} %x_ref.7, bf16[8192,1024]{1,0:T(8,128)(2,1)} %dy_ref.7, bf16[1024,1024]{1,0:T(8,128)(2,1)} %wq_ref.5, ...), custom_call_target="tpu_custom_call" | custom-call | flops 34359738368 | bytes 67108864 | tf_op jit(solution)/shard_map/project1/pallas_call | solution.py:53
  99.3 0.0 all-gather.9.cloned.1.call-update
  99.3 0.2 all-reduce.2.cloned.1.call-start
  99.6 0.0 all-gather.7.cloned.1.call-done
  99.6 39.2 %attend0.1 = (bf16[8192,512]{1,0:T(8,128)(2,1)}, bf16[8192,512]{1,0:T(8,128)(2,1)}, bf16[8192,512]{1,0:T(8,128)(2,1)}, bf16[8192,512]{1,0:T(8,128)(2,1)}) custom-call(bf16[8192,512]{1,0:T(8,128)(2,1)} %get-tuple-element.36.q_ref, bf16[8192,512]{1,0:T(8,128)(2,1)} %get-tuple-element.37.k_ref, bf16[8192,512]{1,0:T(8,128)(2,1)} %get-tuple-element.38.v_ref, ...), custom_call_target="tpu_custom_call" | custom-call | flops 34359738368 | bytes 67108864 | tf_op jit(solution)/shard_map/attend0/pallas_call | solution.py:122
  138.8 43.8 %wgrad0.1 = f32[4,1024,512]{2,1,0:T(8,128)} custom-call(bf16[8192,1024]{1,0:T(8,128)(2,1)} %x_ref.7, bf16[8192,1024]{1,0:T(8,128)(2,1)} %dy_ref.7, bf16[8192,512]{1,0:T(8,128)(2,1)} %get-tuple-element.41.o_ref.o0_ref, bf16[8192,512]{1,0:T(8,128)(2,1)} %get-tuple-element.50.dq0_ref.dq_ref, bf16[8192,512]{1,0:T(8,128)(2,1)} %get-tuple-element.52.dk0_ref.dk_ref, ...), custom_call_target="tpu_custom_call" | custom-call | flops 34359738368 | bytes 67108864 | tf_op jit(solution)/shard_map/wgrad0/pallas_call | solution.py:154
  182.6 0.0 all-reduce.2.cloned.1.call-update
  182.6 0.3 all-gather.11.cloned.1.call-start
  182.9 0.0 all-gather.9.cloned.1.call-done
  182.9 39.2 %attend1.1 = (bf16[8192,512]{1,0:T(8,128)(2,1)}, bf16[8192,512]{1,0:T(8,128)(2,1)}, bf16[8192,512]{1,0:T(8,128)(2,1)}, bf16[8192,512]{1,0:T(8,128)(2,1)}) custom-call(bf16[8192,512]{1,0:T(8,128)(2,1)} %get-tuple-element.42.q_ref, bf16[8192,512]{1,0:T(8,128)(2,1)} %get-tuple-element.43.k_ref, bf16[8192,512]{1,0:T(8,128)(2,1)} %get-tuple-element.44.v_ref, ...), custom_call_target="tpu_custom_call" | custom-call | flops 34359738368 | bytes 67108864 | tf_op jit(solution)/shard_map/attend1/pallas_call | solution.py:122
  222.1 43.8 %wgrad1.1 = f32[4,1024,512]{2,1,0:T(8,128)} custom-call(bf16[8192,1024]{1,0:T(8,128)(2,1)} %x_ref.7, bf16[8192,1024]{1,0:T(8,128)(2,1)} %dy_ref.7, bf16[8192,512]{1,0:T(8,128)(2,1)} %get-tuple-element.47.o_ref.o1_ref, bf16[8192,512]{1,0:T(8,128)(2,1)} %get-tuple-element.51.dq_ref.dq1_ref, bf16[8192,512]{1,0:T(8,128)(2,1)} %get-tuple-element.53.dk_ref.dk1_ref, ...), custom_call_target="tpu_custom_call" | custom-call | flops 34359738368 | bytes 67108864 | tf_op jit(solution)/shard_map/wgrad1/pallas_call | solution.py:154
  265.9 74.5 %reduce_beside.1 = (f32[8192,1024]{1,0:T(8,128)}, f32[2,256,512]{2,1,0:T(8,128)}) custom-call(bf16[8192,512]{1,0:T(8,128)(2,1)} %get-tuple-element.50.dq0_ref.dq_ref, bf16[8192,512]{1,0:T(8,128)(2,1)} %get-tuple-element.51.dq_ref.dq1_ref, bf16[8192,512]{1,0:T(8,128)(2,1)} %get-tuple-element.52.dk0_ref.dk_ref, ...), custom_call_target="tpu_custom_call" | custom-call | flops 34359738368 | bytes 67108864 | tf_op jit(solution)/shard_map/reduce_beside/pallas_call | solution.py:250
  340.4 0.0 all-gather.11.cloned.1.call-update
  340.4 0.0 all-reduce.2.cloned.1.call-done.grad_ref
  340.5 48.8 %back_project.1 = (bf16[8192,1024]{1,0:T(8,128)(2,1)}, bf16[8192,1024]{1,0:T(8,128)(2,1)}, f32[1024,1024]{1,0:T(8,128)}, f32[1024,1024]{1,0:T(8,128)}, f32[1024,1024]{1,0:T(8,128)}, /*index=5*/f32[1024,1024]{1,0:T(8,128)}) custom-call(bf16[8192,512]{1,0:T(8,128)(2,1)} %get-tuple-element.41.o_ref.o0_ref, bf16[8192,512]{1,0:T(8,128)(2,1)} %get-tuple-element.47.o_ref.o1_ref, ...), custom_call_target="tpu_custom_call" | custom-call | flops 34359738368 | bytes 100663296 | tf_op jit(solution)/shard_map/back_project/pallas_call | solution.py:281
  389.3 0.0 all-gather.11.cloned.1.call-done
  389.3 7.0 %place.1 = (f32[1024,1024]{1,0:T(8,128)}, f32[1024,1024]{1,0:T(8,128)}, f32[1024,1024]{1,0:T(8,128)}, f32[1024,1024]{1,0:T(8,128)}) custom-call(f32[8,2,256,512]{3,2,1,0:T(8,128)} %bitcast.4, f32[8,2,256,512]{3,2,1,0:T(8,128)} %bitcast.5, f32[8,2,256,512]{3,2,1,0:T(8,128)} %bitcast.6, ...), custom_call_target="tpu_custom_call", output_to_operand_aliasing={{0}: (4, {}), {1}: (5, {}), {2}: (6, {}), {3}: (7, {})} | custom-call | bytes 16777216 | tf_op jit(solution)/shard_map/place/pallas_call | solution.py:307
Async XLA Ops:
  7.2 92.4 %all-gather.7.cloned.1.call-start = ((), (), s32[]{:S(2)}) async-start(), calls=%async_computation.1 | async-start | bytes 4718592 | tf_op jit(solution)/shard_map/all_gather | solution.py:327
  53.2 129.6 %all-gather.9.cloned.1.call-start = ((), (), s32[]{:S(2)}) async-start(), calls=%async_computation.2 | async-start | bytes 4718592 | tf_op jit(solution)/shard_map/all_gather | solution.py:327
  99.3 241.1 %all-reduce.2.cloned.1.call-start = ((), (), s32[]{:S(2)}) async-start(), calls=%async_computation | async-start | bytes 16777216 | tf_op jit(solution)/shard_map/psum | solution.py:330
  182.6 206.7 %all-gather.11.cloned.1.call-start = ((), (), s32[]{:S(2)}) async-start(), calls=%async_computation.3 | async-start | bytes 9437184 | tf_op jit(solution)/shard_map/all_gather | solution.py:335
Sparse Core Ops, SparseCore 0:
  53.4 33.5 all-gather.6
  99.5 33.5 all-gather.8
  182.7 132.7 all-reduce.1
  340.5 48.3 all-gather.10

commit v2 on v1

--- a/solution.py
+++ b/solution.py
@@ -10,6 +10,7 @@
 HEAD_DIM = 128
 BLOCK_LEN = 128
 GROUPS = 2
+MARKS = ((2, 0, 0), (4, 1, 0), (8, 0, 1), (13, 1, 1))
 
 F32 = jnp.float32
 BF16 = jnp.bfloat16
@@ -113,22 +114,47 @@
         dv_ref[rows, cols] = pair(at_ref[i], k, g, rb_ref[i]).astype(BF16)
 
 
-def attend(q, k, v, g, totals, scale, group, tile):
+def attend_scatter_kernel(scale, marks, q_ref, k_ref, v_ref, g_ref, tot_ref, grad_ref, o_ref, dq_ref, dk_ref, dv_ref, shard_ref, *scratch):
+    def compute():
+        attn_kernel(scale, q_ref, k_ref, v_ref, g_ref, tot_ref, o_ref, dq_ref, dk_ref, dv_ref, *scratch[:10])
+
+    scatter_beside(marks, grad_ref, shard_ref, *scratch[10:], compute)
+
+
+def attend(q, k, v, g, totals, scale, group, tile, grads=None, marks=None):
     n_rows, cols = q.shape
     heads = cols // HEAD_DIM
     row_spec = pl.BlockSpec((tile, cols), lambda i: (i, 0))
     state = (heads, HEAD_DIM, HEAD_DIM)
     units = (tile // BLOCK_LEN * heads, BLOCK_LEN, BLOCK_LEN)
-    return pl.pallas_call(
-        functools.partial(attn_kernel, scale),
+    body = functools.partial(attn_kernel, scale)
+    in_specs = [row_spec] * 4 + [pl.BlockSpec(totals.shape, lambda i: (0, 0, 0, 0, 0))]
+    out_specs = [row_spec] * 4
+    out_shape = [jax.ShapeDtypeStruct((n_rows, cols), BF16)] * 4
+    scratch_shapes = [pltpu.VMEM(state, F32)] * 2 + [pltpu.VMEM(units, BF16)] * 8
+    operands = [q, k, v, g, totals]
+    params = None
+    if grads is not None:
+        total = grads.shape[0] * grads.shape[1]
+        shard = shard_shape(total, cols)
+        body = functools.partial(attend_scatter_kernel, scale, marks)
+        in_specs.append(pl.BlockSpec(memory_space=pl.ANY))
+        out_specs.append(pl.BlockSpec(shard, lambda i: (0, 0, 0, 0)))
+        out_shape.append(jax.ShapeDtypeStruct(shard, F32))
+        scratch_shapes += scatter_scratch(total, cols)
+        operands.append(grads.reshape(total, cols))
+        params = pltpu.CompilerParams(collective_id=1, has_side_effects=True)
+    return pl.pallas_call(
+        body,
         grid=(n_rows // tile,),
-        in_specs=[row_spec] * 4 + [pl.BlockSpec(totals.shape, lambda i: (0, 0, 0, 0, 0))],
-        out_specs=[row_spec] * 4,
-        out_shape=[jax.ShapeDtypeStruct((n_rows, cols), BF16)] * 4,
-        scratch_shapes=[pltpu.VMEM(state, F32)] * 2 + [pltpu.VMEM(units, BF16)] * 8,
+        in_specs=in_specs,
+        out_specs=out_specs,
+        out_shape=out_shape,
+        scratch_shapes=scratch_shapes,
+        compiler_params=params,
         cost_estimate=pl.CostEstimate(flops=64 * n_rows * cols * HEAD_DIM, bytes_accessed=16 * n_rows * cols, transcendentals=0),
         name=f"attend{group}",
-    )(q, k, v, g, totals)
+    )(*operands)
 
 
 def wgrad_kernel(x_ref, dy_ref, o_ref, dq_ref, dk_ref, dv_ref, grad_ref):
@@ -173,13 +199,29 @@
     lax.fori_loop(0, src.shape[0] // step, body, 0)
 
 
-def reduce_kernel(marks, dq0_ref, dq1_ref, dk0_ref, dk1_ref, wq_ref, wk_ref, grad_ref, part_ref, shard_ref, own, got, got_x, got_y, end_x, end_y, send_sem, recv_sem, local_sem):
+CHUNKS = 2
+
+
+def scatter_scratch(total, cols):
+    piece = total // CHUNKS
+    sizes = [piece // part for part in (2, 2, 8, 8, 16, 16) for _ in range(CHUNKS)]
+    return [pltpu.VMEM((size, cols), F32) for size in sizes] + [pltpu.SemaphoreType.DMA((5 * CHUNKS,))] * 2 + [pltpu.SemaphoreType.DMA((CHUNKS,))]
+
+
+def shard_shape(total, cols):
+    return CHUNKS, 2, total // CHUNKS // 16, cols
+
+
+def scatter_beside(marks, grad_ref, shard_ref, *rest):
+    scratch, (send_sem, recv_sem, local_sem, compute) = rest[:-4], rest[-4:]
+    own, got, got_x, got_y, end_x, end_y = (scratch[i * CHUNKS:(i + 1) * CHUNKS] for i in range(6))
     step = pl.program_id(0)
     me = lax.axis_index("sp")
     core, x, y = me % 2, (me // 2) % 2, (me // 4) % 2
     peer_core, peer_x, peer_y = me + 1 - 2 * core, me + 2 - 4 * x, me + 4 - 8 * y
-    half = own.shape[0]
+    half = own[0].shape[0]
     quarter, eighth, last = half // 2, half // 4, half // 8
+    keep_x, keep_y = x * eighth, quarter + y * eighth
 
     def rows(ref, start, size):
         return ref.at[pl.ds(pl.multiple_of(start, last), size), :]
@@ -187,13 +229,41 @@
     def remote(i, src, dst, peer):
         return pltpu.make_async_remote_copy(src_ref=src, dst_ref=dst, send_sem=send_sem.at[i], recv_sem=recv_sem.at[i], device_id={"sp": peer}, device_id_type=pl.DeviceIdType.MESH)
 
-    keep_x, keep_y = x * eighth, quarter + y * eighth
-    swap = remote(0, rows(grad_ref, (1 - core) * half, half), got, peer_core)
-    local = pltpu.make_async_copy(rows(grad_ref, core * half, half), own, local_sem)
-    first_x = remote(1, rows(own, (1 - x) * eighth, eighth), got_x, peer_x)
-    first_y = remote(2, rows(own, quarter + (1 - y) * eighth, eighth), got_y, peer_y)
-    second_x = remote(3, rows(own, keep_x + (1 - y) * last, last), end_x, peer_y)
-    second_y = remote(4, rows(own, keep_y + (1 - x) * last, last), end_y, peer_x)
+    def local(c):
+        return pltpu.make_async_copy(rows(grad_ref, (2 * c + core) * half, half), own[c], local_sem.at[c])
+
+    def copies(c, hop):
+        if hop == 0:
+            return (remote(5 * c, rows(grad_ref, (2 * c + 1 - core) * half, half), got[c], peer_core),)
+        if hop == 1:
+            return (remote(5 * c + 1, rows(own[c], (1 - x) * eighth, eighth), got_x[c], peer_x),
+                    remote(5 * c + 2, rows(own[c], quarter + (1 - y) * eighth, eighth), got_y[c], peer_y))
+        return (remote(5 * c + 3, rows(own[c], keep_x + (1 - y) * last, last), end_x[c], peer_y),
+                remote(5 * c + 4, rows(own[c], keep_y + (1 - x) * last, last), end_y[c], peer_x))
+
+    def start(c, hop):
+        for copy in copies(c, hop):
+            copy.start()
+
+    def finish(c, hop):
+        if hop == 0:
+            local(c).wait()
+        for copy in copies(c, hop):
+            copy.wait()
+        if hop == 0:
+            add_rows(own[c], 0, got[c])
+        elif hop == 1:
+            add_rows(own[c], keep_x, got_x[c])
+            add_rows(own[c], keep_y, got_y[c])
+        else:
+            for i, (at, end) in enumerate(((keep_x + y * last, end_x[c]), (keep_y + x * last, end_y[c]))):
+                shard_ref[c, i] = own[c][pl.ds(pl.multiple_of(at, last), last), :] + end[...]
+
+    def go_on(c, hop):
+        if hop == 0 and c + 1 < CHUNKS:
+            start(c + 1, 0)
+        if hop < 2:
+            start(c, hop + 1)
 
     @pl.when(step == 0)
     def _():
@@ -201,42 +271,35 @@
         for peer in (peer_core, peer_x, peer_y):
             pl.semaphore_signal(barrier, inc=1, device_id={"sp": peer}, device_id_type=pl.DeviceIdType.MESH)
         pl.semaphore_wait(barrier, 3)
-        swap.start()
-        local.start()
-
-    @pl.when(step == marks[0])
-    def _():
-        local.wait()
-        swap.wait()
-        add_rows(own, 0, got)
-
-    @pl.when(step == marks[1])
-    def _():
-        first_x.wait()
-        first_y.wait()
-        add_rows(own, keep_x, got_x)
-        add_rows(own, keep_y, got_y)
-
-    dq = jnp.concatenate([dq0_ref[...], dq1_ref[...]], axis=1)
-    dk = jnp.concatenate([dk0_ref[...], dk1_ref[...]], axis=1)
-    part_ref[...] = dot_nt(dq, wq_ref[...]) + dot_nt(dk, wk_ref[...])
-
-    @pl.when(step == marks[0])
-    def _():
-        first_x.start()
-        first_y.start()
-
-    @pl.when(step == marks[1])
-    def _():
-        second_x.start()
-        second_y.start()
+        start(0, 0)
+        for c in range(CHUNKS):
+            local(c).start()
+
+    for at, c, hop in marks:
+        pl.when(step == at)(functools.partial(finish, c, hop))
+
+    compute()
+
+    for at, c, hop in marks:
+        pl.when(step == at)(functools.partial(go_on, c, hop))
 
     @pl.when(step == pl.num_programs(0) - 1)
     def _():
-        second_x.wait()
-        second_y.wait()
-        shard_ref[0] = own[pl.ds(pl.multiple_of(keep_x + y * last, last), last), :] + end_x[...]
-        shard_ref[1] = own[pl.ds(pl.multiple_of(keep_y + x * last, last), last), :] + end_y[...]
+        met = [mark[1:] for mark in marks]
+        for hop in (1, 2):
+            for c in range(CHUNKS):
+                if (c, hop) not in met:
+                    finish(c, hop)
+                    go_on(c, hop)
+
+
+def reduce_kernel(marks, dq0_ref, dq1_ref, dk0_ref, dk1_ref, wq_ref, wk_ref, grad_ref, part_ref, shard_ref, *scratch):
+    def compute():
+        dq = jnp.concatenate([dq0_ref[...], dq1_ref[...]], axis=1)
+        dk = jnp.concatenate([dk0_ref[...], dk1_ref[...]], axis=1)
+        part_ref[...] = dot_nt(dq, wq_ref[...]) + dot_nt(dk, wk_ref[...])
+
+    scatter_beside(marks, grad_ref, shard_ref, *scratch, compute)
 
 
 def reduce_beside(parts, w_q, w_k, grads, tile, marks):
@@ -245,70 +308,77 @@
     total = grads.shape[0] * grads.shape[1]
     half = pl.BlockSpec((tile, cols), lambda i: (i, 0))
     weight = pl.BlockSpec((dim, dim), lambda i: (0, 0))
-    shard = (2, total // 16, cols)
-    sizes = [total // 2, total // 2, total // 8, total // 8, total // 16, total // 16]
+    shard = shard_shape(total, cols)
     return pl.pallas_call(
         functools.partial(reduce_kernel, marks),
         grid=(n_rows // tile,),
         in_specs=[half] * 4 + [weight] * 2 + [pl.BlockSpec(memory_space=pl.ANY)],
-        out_specs=[pl.BlockSpec((tile, dim), lambda i: (i, 0)), pl.BlockSpec(shard, lambda i: (0, 0, 0))],
+        out_specs=[pl.BlockSpec((tile, dim), lambda i: (i, 0)), pl.BlockSpec(shard, lambda i: (0, 0, 0, 0))],
         out_shape=[jax.ShapeDtypeStruct((n_rows, dim), F32), jax.ShapeDtypeStruct(shard, F32)],
-        scratch_shapes=[pltpu.VMEM((size, cols), F32) for size in sizes] + [pltpu.SemaphoreType.DMA((5,))] * 2 + [pltpu.SemaphoreType.DMA],
+        scratch_shapes=scatter_scratch(total, cols),
         compiler_params=pltpu.CompilerParams(collective_id=0, has_side_effects=True),
         cost_estimate=pl.CostEstimate(flops=4 * n_rows * dim * dim, bytes_accessed=8 * n_rows * dim, transcendentals=0),
         name="reduce_beside",
     )(*parts, w_q, w_k, grads.reshape(total, cols))
 
 
-def out_kernel(o0_ref, o1_ref, dv0_ref, dv1_ref, part_ref, wo_ref, wv_ref, grad_ref, y_ref, dx_ref, gq_ref, gk_ref, gv_ref, go_ref):
+def shard_specs(rows, cols, per_piece):
+    def source(slot):
+        def index(i):
+            piece = i // per_piece
+            part, hi, lo = piece // 4, (piece // 2) % 2, piece % 2
+            x = hi + part * (lo - hi)
+            y = lo + part * (hi - lo)
+            return (y * 2 + x) * 2 + slot % 2, slot // 2, part, i % per_piece, 0
+        return index
+
+    return [pl.BlockSpec((1, 1, 1, rows, cols), source(slot)) for slot in range(4)]
+
+
+def grad_specs(rows, cols, group):
+    down = cols // rows
+    return [pl.BlockSpec((rows, cols), lambda i: (i, group))] * 3 + [pl.BlockSpec((rows, cols), lambda i: (group * down + i % down, i // down))]
+
+
+def out_kernel(o0_ref, o1_ref, dv0_ref, dv1_ref, part_ref, wo_ref, wv_ref, s0_ref, s1_ref, s2_ref, s3_ref, y_ref, dx_ref, gq_ref, gk_ref, gv_ref, go_ref):
     y_ref[...] = dot_nn(jnp.concatenate([o0_ref[...], o1_ref[...]], axis=1), wo_ref[...]).astype(BF16)
     dv = jnp.concatenate([dv0_ref[...], dv1_ref[...]], axis=1)
     dx_ref[...] = (part_ref[...] + dot_nt(dv, wv_ref[...])).astype(BF16)
-    for i, ref in enumerate((gq_ref, gk_ref, gv_ref, go_ref)):
-        ref[...] = grad_ref[i]
-
-
-def back_project(parts, partial, w_o, w_v, grads, tile):
+    for src, dst in ((s0_ref, gq_ref), (s1_ref, gk_ref), (s2_ref, gv_ref), (s3_ref, go_ref)):
+        dst[...] = src[0, 0, 0]
+
+
+def back_project(parts, partial, w_o, w_v, gathered, tile):
     n_rows, cols = parts[0].shape
     dim = w_o.shape[1]
     steps = n_rows // tile
     piece = dim // steps
-    down = cols // piece
     half = pl.BlockSpec((tile, cols), lambda i: (i, 0))
     weight = pl.BlockSpec((dim, dim), lambda i: (0, 0))
     row_out = pl.BlockSpec((tile, dim), lambda i: (i, 0))
-    left = pl.BlockSpec((piece, cols), lambda i: (i, 0))
     return pl.pallas_call(
         out_kernel,
         grid=(steps,),
-        in_specs=[half] * 4 + [row_out] + [weight] * 2 + [pl.BlockSpec((4, piece, cols), lambda i: (0, i, 0))],
-        out_specs=[row_out] * 2 + [left] * 3 + [pl.BlockSpec((piece, cols), lambda i: (i % down, i // down))],
+        in_specs=[half] * 4 + [row_out] + [weight] * 2 + shard_specs(piece, cols, steps // 8),
+        out_specs=[row_out] * 2 + grad_specs(piece, cols, 0),
         out_shape=[jax.ShapeDtypeStruct((n_rows, dim), BF16)] * 2 + [jax.ShapeDtypeStruct((dim, dim), F32)] * 4,
         cost_estimate=pl.CostEstimate(flops=4 * n_rows * dim * dim, bytes_accessed=12 * n_rows * dim, transcendentals=0),
         name="back_project",
-    )(*parts, partial, w_o, w_v, grads)
+    )(*parts, partial, w_o, w_v, *[gathered] * 4)
 
 
 def place_kernel(s0_ref, s1_ref, s2_ref, s3_ref, a0_ref, a1_ref, a2_ref, a3_ref, gq_ref, gk_ref, gv_ref, go_ref):
     for src, dst in ((s0_ref, gq_ref), (s1_ref, gk_ref), (s2_ref, gv_ref), (s3_ref, go_ref)):
-        dst[...] = src[0, 0]
+        dst[...] = src[0, 0, 0]
 
 
 def place(gathered, grads):
-    piece, cols = gathered.shape[2:]
-    down = cols // piece
-
-    def source(slot):
-        if slot % 2:
-            return lambda i: (i * 2 + slot // 2, 1, 0, 0)
-        return lambda i: (((i % 2) * 2 + i // 2) * 2 + slot // 2, 0, 0, 0)
-
-    right = pl.BlockSpec((piece, cols), lambda i: (i, 1))
+    piece, cols = gathered.shape[3:]
     return pl.pallas_call(
         place_kernel,
-        grid=(4,),
-        in_specs=[pl.BlockSpec((1, 1, piece, cols), source(slot)) for slot in range(4)] + [pl.BlockSpec(memory_space=pl.ANY)] * 4,
-        out_specs=[right] * 3 + [pl.BlockSpec((piece, cols), lambda i: (down + i % down, i // down))],
+        grid=(8,),
+        in_specs=shard_specs(piece, cols, 1) + [pl.BlockSpec(memory_space=pl.ANY)] * 4,
+        out_specs=grad_specs(piece, cols, 1),
         out_shape=[jax.ShapeDtypeStruct(g.shape, g.dtype) for g in grads],
         input_output_aliases={4 + i: i for i in range(4)},
         cost_estimate=pl.CostEstimate(flops=0, bytes_accessed=8 * gathered.size, transcendentals=0),
@@ -327,13 +397,14 @@
         gathered = [lax.all_gather(p[4], "sp") for p in projected]
         parts = [None] * GROUPS
         parts[0] = attend(*projected[0][:4], gathered[0], scale, 0, 512)
-        first = lax.psum(weight_grads(tokens, grad_y, *parts[0], 0, 1024), "sp")
-        parts[1] = attend(*projected[1][:4], gathered[1], scale, 1, 512)
+        first = weight_grads(tokens, grad_y, *parts[0], 0, 1024)
+        *parts[1], shard0 = attend(*projected[1][:4], gathered[1], scale, 1, 512, first, MARKS)
+        shards0 = lax.all_gather(shard0, "sp")
         second = weight_grads(tokens, grad_y, *parts[1], 1, 1024)
         o, dq, dk, dv = zip(*parts)
-        partial, shard = reduce_beside(dq + dk, w_q, w_k, second, 512, (3, 13))
-        shards = lax.all_gather(shard, "sp")
-        out_y, grad_x, *grads = back_project(o + dv, partial, w_o, w_v, first, 512)
-        return (out_y, grad_x) + tuple(place(shards, grads))
+        partial, shard1 = reduce_beside(dq + dk, w_q, w_k, second, 512, MARKS)
+        shards1 = lax.all_gather(shard1, "sp")
+        out_y, grad_x, *grads = back_project(o + dv, partial, w_o, w_v, shards0, 512)
+        return (out_y, grad_x) + tuple(place(shards1, grads))
 
     return jax.shard_map(local_layer, mesh=mesh, in_specs=(row_spec, P(), P(), P(), P(), row_spec), out_specs=(row_spec, row_spec, grad_spec, grad_spec, grad_spec, grad_spec), check_vma=False)

time: 404 us -> 395 us (0.978)
  Pallas kernels: 388 us -> 379 us
    pallas_call x1, Pallas kernels: 74.5 us -> 50.3 us  [reduce_beside(): pl.pallas_call(functools.partial(reduce_kernel, marks), grid=(n_rows // t...]
    pallas_call x3, Pallas kernels: 85.4 us -> 99.2 us  [the longest x2 90.3 us: attend(): pl.pallas_call(body, grid=(n_rows // tile,), in_specs=in_specs, out_specs...]
  transfers between devices with their start and end apart: 4 -> 4, of which waited for: 0 -> 0; matrix products, arithmetic and copies ran while one was open for 0% -> 0% of each run, Pallas kernels for 83% -> 69%
where the time goes in v2:
time: 395 us; the launch traced here: 394 us
  Pallas kernels  379 us (96%)
  between operations  13.8 us (3%)
    pallas_call x2, Pallas kernels, project(): pl.pallas_call(proj_kernel, grid=(n_rows // tile,), in_specs=[row_in, row...  92 us
    pallas_call x2, Pallas kernels, attend(): pl.pallas_call(body, grid=(n_rows // tile,), in_specs=in_specs, out_specs...  90.3 us
    pallas_call x2, Pallas kernels, weight_grads(): pl.pallas_call(wgrad_kernel, grid=(n_rows // tile,), in_specs=[wide, wide...  87.7 us
    pallas_call x1, Pallas kernels, reduce_beside(): pl.pallas_call(functools.partial(reduce_kernel, marks), grid=(n_rows // t...  50.3 us
    pallas_call x1, Pallas kernels, back_project(): pl.pallas_call(out_kernel, grid=(steps,), in_specs=[half] * 4 + [row_out]...  50.2 us
    pallas_call x1, Pallas kernels, place(): pl.pallas_call(place_kernel, grid=(8,), in_specs=shard_specs(piece, cols,...  8.83 us
  transfers between devices with their start and end apart: 4, of which 0 were waited for; matrix products, arithmetic and copies ran while one was open for 0% of the time, Pallas kernels for 69%

profile of v2, /device:TPU:0, one launch (start us, length us, event | category | flops | bytes accessed | tf_op | source)
XLA Modules:
  0.0 393.9 jit_solution(1536859103063469648)
XLA Ops:
  7.2 0.0 all-gather.9.cloned.1.call-start
  7.2 46.0 %project0.1 = (bf16[8192,512]{1,0:T(8,128)(2,1)}, bf16[8192,512]{1,0:T(8,128)(2,1)}, bf16[8192,512]{1,0:T(8,128)(2,1)}, bf16[8192,512]{1,0:T(8,128)(2,1)}, f32[2,4,128,128]{3,2,1,0:T(8,128)}) custom-call(bf16[8192,1024]{1,0:T(8,128)(2,1)} %x_ref.7, bf16[8192,1024]{1,0:T(8,128)(2,1)} %dy_ref.7, bf16[1024,1024]{1,0:T(8,128)(2,1)} %wq_ref.5, ...), custom_call_target="tpu_custom_call" | custom-call | flops 34359738368 | bytes 67108864 | tf_op jit(solution)/shard_map/project0/pallas_call | solution.py:54
  53.2 0.0 all-gather.9.cloned.1.call-update
  53.2 0.0 all-gather.11.cloned.1.call-start
  53.3 46.0 %project1.1 = (bf16[8192,512]{1,0:T(8,128)(2,1)}, bf16[8192,512]{1,0:T(8,128)(2,1)}, bf16[8192,512]{1,0:T(8,128)(2,1)}, bf16[8192,512]{1,0:T(8,128)(2,1)}, f32[2,4,128,128]{3,2,1,0:T(8,128)}) custom-call(bf16[8192,1024]{1,0:T(8,128)(2,1)} %x_ref.7, bf16[8192,1024]{1,0:T(8,128)(2,1)} %dy_ref.7, bf16[1024,1024]{1,0:T(8,128)(2,1)} %wq_ref.5, ...), custom_call_target="tpu_custom_call" | custom-call | flops 34359738368 | bytes 67108864 | tf_op jit(solution)/shard_map/project1/pallas_call | solution.py:54
  99.3 0.0 all-gather.11.cloned.1.call-update
  99.3 0.2 all-gather.13.cloned.1.call-start
  99.6 0.0 all-gather.9.cloned.1.call-done
  99.6 39.2 %attend0.1 = (bf16[8192,512]{1,0:T(8,128)(2,1)}, bf16[8192,512]{1,0:T(8,128)(2,1)}, bf16[8192,512]{1,0:T(8,128)(2,1)}, bf16[8192,512]{1,0:T(8,128)(2,1)}) custom-call(bf16[8192,512]{1,0:T(8,128)(2,1)} %get-tuple-element.37.q_ref, bf16[8192,512]{1,0:T(8,128)(2,1)} %get-tuple-element.38.k_ref, bf16[8192,512]{1,0:T(8,128)(2,1)} %get-tuple-element.39.v_ref, ...), custom_call_target="tpu_custom_call" | custom-call | flops 34359738368 | bytes 67108864 | tf_op jit(solution)/shard_map/attend0/pallas_call | solution.py:147
  138.8 43.9 %wgrad0.1 = f32[4,1024,512]{2,1,0:T(8,128)} custom-call(bf16[8192,1024]{1,0:T(8,128)(2,1)} %x_ref.7, bf16[8192,1024]{1,0:T(8,128)(2,1)} %dy_ref.7, bf16[8192,512]{1,0:T(8,128)(2,1)} %get-tuple-element.42.o_ref.o0_ref, bf16[8192,512]{1,0:T(8,128)(2,1)} %get-tuple-element.48.dq_ref.dq0_ref, bf16[8192,512]{1,0:T(8,128)(2,1)} %get-tuple-element.49.dk_ref.dk0_ref, ...), custom_call_target="tpu_custom_call" | custom-call | flops 34359738368 | bytes 67108864 | tf_op jit(solution)/shard_map/wgrad0/pallas_call | solution.py:180
  182.7 0.0 all-gather.11.cloned.1.call-done
  182.7 51.1 %attend1.1 = (bf16[8192,512]{1,0:T(8,128)(2,1)}, bf16[8192,512]{1,0:T(8,128)(2,1)}, bf16[8192,512]{1,0:T(8,128)(2,1)}, bf16[8192,512]{1,0:T(8,128)(2,1)}, f32[2,2,128,512]{3,2,1,0:T(8,128)}) custom-call(bf16[8192,512]{1,0:T(8,128)(2,1)} %get-tuple-element.43.q_ref, bf16[8192,512]{1,0:T(8,128)(2,1)} %get-tuple-element.44.k_ref, ...), custom_call_target="tpu_custom_call" | custom-call | flops 34359738368 | bytes 67108864 | tf_op jit(solution)/shard_map/attend1/pallas_call | solution.py:147
  233.8 0.0 all-gather.13.cloned.1.call-update
  233.8 0.3 all-gather.15.cloned.1.call-start
  234.1 43.9 %wgrad1.1 = f32[4,1024,512]{2,1,0:T(8,128)} custom-call(bf16[8192,1024]{1,0:T(8,128)(2,1)} %x_ref.7, bf16[8192,1024]{1,0:T(8,128)(2,1)} %dy_ref.7, bf16[8192,512]{1,0:T(8,128)(2,1)} %get-tuple-element.51.o_ref.o1_ref, bf16[8192,512]{1,0:T(8,128)(2,1)} %get-tuple-element.53.dq_ref.dq1_ref, bf16[8192,512]{1,0:T(8,128)(2,1)} %get-tuple-element.54.dk_ref.dk1_ref, ...), custom_call_target="tpu_custom_call" | custom-call | flops 34359738368 | bytes 67108864 | tf_op jit(solution)/shard_map/wgrad1/pallas_call | solution.py:180
  277.9 50.3 %reduce_beside.1 = (f32[8192,1024]{1,0:T(8,128)}, f32[2,2,128,512]{3,2,1,0:T(8,128)}) custom-call(bf16[8192,512]{1,0:T(8,128)(2,1)} %get-tuple-element.48.dq_ref.dq0_ref, bf16[8192,512]{1,0:T(8,128)(2,1)} %get-tuple-element.53.dq_ref.dq1_ref, bf16[8192,512]{1,0:T(8,128)(2,1)} %get-tuple-element.49.dk_ref.dk0_ref, ...), custom_call_target="tpu_custom_call" | custom-call | flops 34359738368 | bytes 67108864 | tf_op jit(solution)/shard_map/reduce_beside/pallas_call | solution.py:312
  328.3 0.0 all-gather.15.cloned.1.call-update
  328.3 0.0 all-gather.13.cloned.1.call-done
  328.3 50.2 %back_project.1 = (bf16[8192,1024]{1,0:T(8,128)(2,1)}, bf16[8192,1024]{1,0:T(8,128)(2,1)}, f32[1024,1024]{1,0:T(8,128)}, f32[1024,1024]{1,0:T(8,128)}, f32[1024,1024]{1,0:T(8,128)}, /*index=5*/f32[1024,1024]{1,0:T(8,128)}) custom-call(bf16[8192,512]{1,0:T(8,128)(2,1)} %get-tuple-element.42.o_ref.o0_ref, bf16[8192,512]{1,0:T(8,128)(2,1)} %get-tuple-element.51.o_ref.o1_ref, ...), custom_call_target="tpu_custom_call" | custom-call | flops 34359738368 | bytes 100663296 | tf_op jit(solution)/shard_map/back_project/pallas_call | solution.py:359
  378.5 0.0 all-gather.15.cloned.1.call-done
  378.5 8.8 %place.1 = (f32[1024,1024]{1,0:T(8,128)}, f32[1024,1024]{1,0:T(8,128)}, f32[1024,1024]{1,0:T(8,128)}, f32[1024,1024]{1,0:T(8,128)}) custom-call(f32[8,2,2,128,512]{4,3,2,1,0:T(8,128)} %bitcast.6, f32[8,2,2,128,512]{4,3,2,1,0:T(8,128)} %bitcast.7, ...), custom_call_target="tpu_custom_call", output_to_operand_aliasing={{0}: (4, {}), {1}: (5, {}), {2}: (6, {}), {3}: (7, {})} | custom-call | bytes 16777216 | tf_op jit(solution)/shard_map/place/pallas_call | solution.py:377
Async XLA Ops:
  7.2 92.4 %all-gather.9.cloned.1.call-start = ((), (), s32[]{:S(2)}) async-start(), calls=%async_computation | async-start | bytes 4718592 | tf_op jit(solution)/shard_map/all_gather | solution.py:397
  53.2 129.4 %all-gather.11.cloned.1.call-start = ((), (), s32[]{:S(2)}) async-start(), calls=%async_computation.1 | async-start | bytes 4718592 | tf_op jit(solution)/shard_map/all_gather | solution.py:397
  99.3 229.0 %all-gather.13.cloned.1.call-start = ((), (), s32[]{:S(2)}) async-start(), calls=%async_computation.2 | async-start | bytes 9437184 | tf_op jit(solution)/shard_map/all_gather | solution.py:402
  233.8 144.7 %all-gather.15.cloned.1.call-start = ((), (), s32[]{:S(2)}) async-start(), calls=%async_computation.3 | async-start | bytes 9437184 | tf_op jit(solution)/shard_map/all_gather | solution.py:406
Sparse Core Ops, SparseCore 0:
  53.4 33.5 all-gather.8
  99.5 33.5 all-gather.10
  233.9 48.3 all-gather.12
  328.4 48.3 all-gather.14

commit v3 on v2

--- a/solution.py
+++ b/solution.py
@@ -10,7 +10,7 @@
 HEAD_DIM = 128
 BLOCK_LEN = 128
 GROUPS = 2
-MARKS = ((2, 0, 0), (4, 1, 0), (8, 0, 1), (13, 1, 1))
+MARKS = ((2, 0, 0), (5, 1, 0), (8, 0, 1), (13, 1, 1))
 
 F32 = jnp.float32
 BF16 = jnp.bfloat16
@@ -189,7 +189,7 @@
 
 
 def add_rows(dst, start, src):
-    step = 64
+    step = 128
 
     def body(i, carry):
         there = pl.ds(pl.multiple_of(start + i * step, step), step)
@@ -322,17 +322,18 @@
     )(*parts, w_q, w_k, grads.reshape(total, cols))
 
 
-def shard_specs(rows, cols, per_piece):
-    def source(slot):
-        def index(i):
-            piece = i // per_piece
-            part, hi, lo = piece // 4, (piece // 2) % 2, piece % 2
-            x = hi + part * (lo - hi)
-            y = lo + part * (hi - lo)
-            return (y * 2 + x) * 2 + slot % 2, slot // 2, part, i % per_piece, 0
-        return index
-
-    return [pl.BlockSpec((1, 1, 1, rows, cols), source(slot)) for slot in range(4)]
+def shard_spec(shards, slot, rows, block_of):
+    per_piece = shards.shape[3] // rows
+
+    def index(i):
+        block = block_of(i)
+        piece = block // per_piece
+        part, hi, lo = piece // 4, (piece // 2) % 2, piece % 2
+        x = hi + part * (lo - hi)
+        y = lo + part * (hi - lo)
+        return (y * 2 + x) * 2 + slot % 2, slot // 2, part, block % per_piece, 0
+
+    return pl.BlockSpec((1, 1, 1, rows, shards.shape[4]), index)
 
 
 def grad_specs(rows, cols, group):
@@ -359,7 +360,7 @@
     return pl.pallas_call(
         out_kernel,
         grid=(steps,),
-        in_specs=[half] * 4 + [row_out] + [weight] * 2 + shard_specs(piece, cols, steps // 8),
+        in_specs=[half] * 4 + [row_out] + [weight] * 2 + [shard_spec(gathered, slot, piece, lambda i: i) for slot in range(4)],
         out_specs=[row_out] * 2 + grad_specs(piece, cols, 0),
         out_shape=[jax.ShapeDtypeStruct((n_rows, dim), BF16)] * 2 + [jax.ShapeDtypeStruct((dim, dim), F32)] * 4,
         cost_estimate=pl.CostEstimate(flops=4 * n_rows * dim * dim, bytes_accessed=12 * n_rows * dim, transcendentals=0),
@@ -367,23 +368,30 @@
     )(*parts, partial, w_o, w_v, *[gathered] * 4)
 
 
-def place_kernel(s0_ref, s1_ref, s2_ref, s3_ref, a0_ref, a1_ref, a2_ref, a3_ref, gq_ref, gk_ref, gv_ref, go_ref):
-    for src, dst in ((s0_ref, gq_ref), (s1_ref, gk_ref), (s2_ref, gv_ref), (s3_ref, go_ref)):
-        dst[...] = src[0, 0, 0]
+PLACE_PARTS = 2
+
+
+def place_kernel(*refs):
+    shards, outs = refs[:4 * PLACE_PARTS], refs[4 * PLACE_PARTS + 4:]
+    rows = shards[0].shape[3]
+    for i, shard in enumerate(shards):
+        there = (i % PLACE_PARTS) * rows
+        outs[i // PLACE_PARTS][there:there + rows] = shard[0, 0, 0]
 
 
 def place(gathered, grads):
     piece, cols = gathered.shape[3:]
+    sources = [shard_spec(gathered, slot, piece, lambda i, r=r: i * PLACE_PARTS + r) for slot in range(4) for r in range(PLACE_PARTS)]
     return pl.pallas_call(
         place_kernel,
-        grid=(8,),
-        in_specs=shard_specs(piece, cols, 1) + [pl.BlockSpec(memory_space=pl.ANY)] * 4,
-        out_specs=grad_specs(piece, cols, 1),
+        grid=(8 // PLACE_PARTS,),
+        in_specs=sources + [pl.BlockSpec(memory_space=pl.ANY)] * 4,
+        out_specs=grad_specs(PLACE_PARTS * piece, cols, 1),
         out_shape=[jax.ShapeDtypeStruct(g.shape, g.dtype) for g in grads],
-        input_output_aliases={4 + i: i for i in range(4)},
+        input_output_aliases={len(sources) + i: i for i in range(4)},
         cost_estimate=pl.CostEstimate(flops=0, bytes_accessed=8 * gathered.size, transcendentals=0),
         name="place",
-    )(*[gathered] * 4, *grads)
+    )(*[gathered] * len(sources), *grads)
 
 
 def solution(mesh):

time: 395 us -> 392 us (level)
  transfers between devices with their start and end apart: 4 -> 4, of which waited for: 0 -> 0; matrix products, arithmetic and copies ran while one was open for 0% -> 0% of each run, Pallas kernels for 69% -> 70%
where the time goes in v3:
time: 392 us; the launch traced here: 390 us
  Pallas kernels  376 us (96%)
  between operations  13.8 us (4%)
    pallas_call x2, Pallas kernels, project(): pl.pallas_call(proj_kernel, grid=(n_rows // tile,), in_specs=[row_in, row...  92 us
    pallas_call x2, Pallas kernels, attend(): pl.pallas_call(body, grid=(n_rows // tile,), in_specs=in_specs, out_specs...  90.3 us
    pallas_call x2, Pallas kernels, weight_grads(): pl.pallas_call(wgrad_kernel, grid=(n_rows // tile,), in_specs=[wide, wide...  87.7 us
    pallas_call x1, Pallas kernels, back_project(): pl.pallas_call(out_kernel, grid=(steps,), in_specs=[half] * 4 + [row_out]...  50.2 us
    pallas_call x1, Pallas kernels, reduce_beside(): pl.pallas_call(functools.partial(reduce_kernel, marks), grid=(n_rows // t...  48.5 us
  transfers between devices with their start and end apart: 4, of which 0 were waited for; matrix products, arithmetic and copies ran while one was open for 0% of the time, Pallas kernels for 70%

profile of v3, /device:TPU:0, one launch (start us, length us, event | category | flops | bytes accessed | tf_op | source)
XLA Modules:
  0.0 390.2 jit_solution(18031703174450816685)
XLA Ops:
  7.2 0.0 all-gather.9.cloned.1.call-start
  7.2 46.0 %project0.1 = (bf16[8192,512]{1,0:T(8,128)(2,1)}, bf16[8192,512]{1,0:T(8,128)(2,1)}, bf16[8192,512]{1,0:T(8,128)(2,1)}, bf16[8192,512]{1,0:T(8,128)(2,1)}, f32[2,4,128,128]{3,2,1,0:T(8,128)}) custom-call(bf16[8192,1024]{1,0:T(8,128)(2,1)} %x_ref.7, bf16[8192,1024]{1,0:T(8,128)(2,1)} %dy_ref.7, bf16[1024,1024]{1,0:T(8,128)(2,1)} %wq_ref.5, ...), custom_call_target="tpu_custom_call" | custom-call | flops 34359738368 | bytes 67108864 | tf_op jit(solution)/shard_map/project0/pallas_call | solution.py:54
  53.2 0.0 all-gather.9.cloned.1.call-update
  53.2 0.0 all-gather.11.cloned.1.call-start
  53.3 46.0 %project1.1 = (bf16[8192,512]{1,0:T(8,128)(2,1)}, bf16[8192,512]{1,0:T(8,128)(2,1)}, bf16[8192,512]{1,0:T(8,128)(2,1)}, bf16[8192,512]{1,0:T(8,128)(2,1)}, f32[2,4,128,128]{3,2,1,0:T(8,128)}) custom-call(bf16[8192,1024]{1,0:T(8,128)(2,1)} %x_ref.7, bf16[8192,1024]{1,0:T(8,128)(2,1)} %dy_ref.7, bf16[1024,1024]{1,0:T(8,128)(2,1)} %wq_ref.5, ...), custom_call_target="tpu_custom_call" | custom-call | flops 34359738368 | bytes 67108864 | tf_op jit(solution)/shard_map/project1/pallas_call | solution.py:54
  99.3 0.0 all-gather.11.cloned.1.call-update
  99.3 0.2 all-gather.13.cloned.1.call-start
  99.6 0.0 all-gather.9.cloned.1.call-done
  99.6 39.2 %attend0.1 = (bf16[8192,512]{1,0:T(8,128)(2,1)}, bf16[8192,512]{1,0:T(8,128)(2,1)}, bf16[8192,512]{1,0:T(8,128)(2,1)}, bf16[8192,512]{1,0:T(8,128)(2,1)}) custom-call(bf16[8192,512]{1,0:T(8,128)(2,1)} %get-tuple-element.37.q_ref, bf16[8192,512]{1,0:T(8,128)(2,1)} %get-tuple-element.38.k_ref, bf16[8192,512]{1,0:T(8,128)(2,1)} %get-tuple-element.39.v_ref, ...), custom_call_target="tpu_custom_call" | custom-call | flops 34359738368 | bytes 67108864 | tf_op jit(solution)/shard_map/attend0/pallas_call | solution.py:147
  138.8 43.9 %wgrad0.1 = f32[4,1024,512]{2,1,0:T(8,128)} custom-call(bf16[8192,1024]{1,0:T(8,128)(2,1)} %x_ref.7, bf16[8192,1024]{1,0:T(8,128)(2,1)} %dy_ref.7, bf16[8192,512]{1,0:T(8,128)(2,1)} %get-tuple-element.42.o_ref.o0_ref, bf16[8192,512]{1,0:T(8,128)(2,1)} %get-tuple-element.48.dq_ref.dq0_ref, bf16[8192,512]{1,0:T(8,128)(2,1)} %get-tuple-element.49.dk_ref.dk0_ref, ...), custom_call_target="tpu_custom_call" | custom-call | flops 34359738368 | bytes 67108864 | tf_op jit(solution)/shard_map/wgrad0/pallas_call | solution.py:180
  182.7 0.0 all-gather.11.cloned.1.call-done
  182.7 51.1 %attend1.1 = (bf16[8192,512]{1,0:T(8,128)(2,1)}, bf16[8192,512]{1,0:T(8,128)(2,1)}, bf16[8192,512]{1,0:T(8,128)(2,1)}, bf16[8192,512]{1,0:T(8,128)(2,1)}, f32[2,2,128,512]{3,2,1,0:T(8,128)}) custom-call(bf16[8192,512]{1,0:T(8,128)(2,1)} %get-tuple-element.43.q_ref, bf16[8192,512]{1,0:T(8,128)(2,1)} %get-tuple-element.44.k_ref, ...), custom_call_target="tpu_custom_call" | custom-call | flops 34359738368 | bytes 67108864 | tf_op jit(solution)/shard_map/attend1/pallas_call | solution.py:147
  233.8 0.0 all-gather.13.cloned.1.call-update
  233.8 0.3 all-gather.15.cloned.1.call-start
  234.1 43.9 %wgrad1.1 = f32[4,1024,512]{2,1,0:T(8,128)} custom-call(bf16[8192,1024]{1,0:T(8,128)(2,1)} %x_ref.7, bf16[8192,1024]{1,0:T(8,128)(2,1)} %dy_ref.7, bf16[8192,512]{1,0:T(8,128)(2,1)} %get-tuple-element.51.o_ref.o1_ref, bf16[8192,512]{1,0:T(8,128)(2,1)} %get-tuple-element.53.dq_ref.dq1_ref, bf16[8192,512]{1,0:T(8,128)(2,1)} %get-tuple-element.54.dk_ref.dk1_ref, ...), custom_call_target="tpu_custom_call" | custom-call | flops 34359738368 | bytes 67108864 | tf_op jit(solution)/shard_map/wgrad1/pallas_call | solution.py:180
  277.9 48.5 %reduce_beside.1 = (f32[8192,1024]{1,0:T(8,128)}, f32[2,2,128,512]{3,2,1,0:T(8,128)}) custom-call(bf16[8192,512]{1,0:T(8,128)(2,1)} %get-tuple-element.48.dq_ref.dq0_ref, bf16[8192,512]{1,0:T(8,128)(2,1)} %get-tuple-element.53.dq_ref.dq1_ref, bf16[8192,512]{1,0:T(8,128)(2,1)} %get-tuple-element.49.dk_ref.dk0_ref, ...), custom_call_target="tpu_custom_call" | custom-call | flops 34359738368 | bytes 67108864 | tf_op jit(solution)/shard_map/reduce_beside/pallas_call | solution.py:312
  326.5 0.0 all-gather.15.cloned.1.call-update
  326.5 0.0 all-gather.13.cloned.1.call-done
  326.5 50.2 %back_project.1 = (bf16[8192,1024]{1,0:T(8,128)(2,1)}, bf16[8192,1024]{1,0:T(8,128)(2,1)}, f32[1024,1024]{1,0:T(8,128)}, f32[1024,1024]{1,0:T(8,128)}, f32[1024,1024]{1,0:T(8,128)}, /*index=5*/f32[1024,1024]{1,0:T(8,128)}) custom-call(bf16[8192,512]{1,0:T(8,128)(2,1)} %get-tuple-element.42.o_ref.o0_ref, bf16[8192,512]{1,0:T(8,128)(2,1)} %get-tuple-element.51.o_ref.o1_ref, ...), custom_call_target="tpu_custom_call" | custom-call | flops 34359738368 | bytes 100663296 | tf_op jit(solution)/shard_map/back_project/pallas_call | solution.py:360
  376.7 0.0 all-gather.15.cloned.1.call-done
  376.7 7.0 %place.1 = (f32[1024,1024]{1,0:T(8,128)}, f32[1024,1024]{1,0:T(8,128)}, f32[1024,1024]{1,0:T(8,128)}, f32[1024,1024]{1,0:T(8,128)}) custom-call(f32[8,2,2,128,512]{4,3,2,1,0:T(8,128)} %bitcast.6, f32[8,2,2,128,512]{4,3,2,1,0:T(8,128)} %bitcast.7, ...), custom_call_target="tpu_custom_call", output_to_operand_aliasing={{0}: (8, {}), {1}: (9, {}), {2}: (10, {}), {3}: (11, {})} | custom-call | bytes 16777216 | tf_op jit(solution)/shard_map/place/pallas_call | solution.py:385
Async XLA Ops:
  7.2 92.4 %all-gather.9.cloned.1.call-start = ((), (), s32[]{:S(2)}) async-start(), calls=%async_computation | async-start | bytes 4718592 | tf_op jit(solution)/shard_map/all_gather | solution.py:405
  53.2 129.4 %all-gather.11.cloned.1.call-start = ((), (), s32[]{:S(2)}) async-start(), calls=%async_computation.1 | async-start | bytes 4718592 | tf_op jit(solution)/shard_map/all_gather | solution.py:405
  99.3 227.2 %all-gather.13.cloned.1.call-start = ((), (), s32[]{:S(2)}) async-start(), calls=%async_computation.2 | async-start | bytes 9437184 | tf_op jit(solution)/shard_map/all_gather | solution.py:410
  233.8 142.9 %all-gather.15.cloned.1.call-start = ((), (), s32[]{:S(2)}) async-start(), calls=%async_computation.3 | async-start | bytes 9437184 | tf_op jit(solution)/shard_map/all_gather | solution.py:414
Sparse Core Ops, SparseCore 0:
  53.4 33.5 all-gather.8
  99.5 33.5 all-gather.10
  233.9 48.3 all-gather.12
  326.6 48.3 all-gather.14
